TPU v7x, 16 devices: a whole 2x2x2 slice. The times are simulated.
16 devices in a mesh: node: 2 (over z), local: 8 (over y, x, core).
Axes of the slice: x: 2, y: 2, z: 2, core: 2. Of those that a mesh axis runs over, the one named last changes fastest.
Arguments:
- x: bfloat16 [16, 256, 512], P(('node', 'local'))
- y_cot: bfloat16 [16, 256, 512], P(('node', 'local'))
- ln1_gain: bfloat16 [2, 512], P(None, ('node', 'local'))
- ln1_bias: bfloat16 [2, 512], P(None, ('node', 'local'))
- qkv_weight: bfloat16 [2, 512, 8, 192], P(None, ('node', 'local'))
- qkv_bias: bfloat16 [2, 1536], P(None, ('node', 'local'))
- out_weight: bfloat16 [2, 512, 512], P(None, ('node', 'local'))
- out_bias: bfloat16 [2, 512], P(None, ('node', 'local'))
- ln2_gain: bfloat16 [2, 512], P(None, ('node', 'local'))
- ln2_bias: bfloat16 [2, 512], P(None, ('node', 'local'))
- up_weight: bfloat16 [2, 512, 2048], P(None, ('node', 'local'))
- up_bias: bfloat16 [2, 2048], P(None, ('node', 'local'))
- down_weight: bfloat16 [2, 2048, 512], P(None, ('node', 'local'))
- down_bias: bfloat16 [2, 512], P(None, ('node', 'local'))
Outputs:
- output 1: bfloat16 [16, 256, 512], P(('node', 'local'))
- output 2: bfloat16 [16, 256, 512], P(('node', 'local'))
- output 3: bfloat16 [2, 512], P(None, ('node', 'local'))
- output 4: bfloat16 [2, 512], P(None, ('node', 'local'))
- output 5: bfloat16 [2, 512, 8, 192], P(None, ('node', 'local'))
- output 6: bfloat16 [2, 1536], P(None, ('node', 'local'))
- output 7: bfloat16 [2, 512, 512], P(None, ('node', 'local'))
- output 8: bfloat16 [2, 512], P(None, ('node', 'local'))
- output 9: bfloat16 [2, 512], P(None, ('node', 'local'))
- output 10: bfloat16 [2, 512], P(None, ('node', 'local'))
- output 11: bfloat16 [2, 512, 2048], P(None, ('node', 'local'))
- output 12: bfloat16 [2, 2048], P(None, ('node', 'local'))
- output 13: bfloat16 [2, 2048, 512], P(None, ('node', 'local'))
- output 14: bfloat16 [2, 512], P(None, ('node', 'local'))
All inputs are finite; a program needn't handle non-finite values.
Results may differ from a plain program's by a relative error of at most 0.0164011.
Values are sent between devices in bfloat16 or wider.
A program may use at most 1 GiB of HBM per device.

v0:
```python
import functools
import jax
import jax.numpy as jnp
from jax import lax
from jax.sharding import PartitionSpec as P, NamedSharding

EPSILON = 1e-5


def product(einsum_form, first_op, second_op):
    return jnp.einsum(einsum_form, first_op, second_op, preferred_element_type=jnp.float32)


def rope_tables(seq_len, rot_dim):
    inv_freq = 1.0 / (10000.0 ** (jnp.arange(0, rot_dim, 2, dtype=jnp.float32) / rot_dim))
    angles = jnp.arange(seq_len, dtype=jnp.float32)[:, None] * inv_freq[None, :]
    angles = jnp.concatenate([angles, angles], axis=-1)
    return jnp.cos(angles), jnp.sin(angles)


def norm_pair(hidden32, gain_attn, bias_attn, gain_mlp, bias_mlp):
    center = hidden32 - jnp.mean(hidden32, axis=-1, keepdims=True)
    scaled = center * lax.rsqrt(jnp.mean(center * center, axis=-1, keepdims=True) + EPSILON)
    return ((scaled * gain_attn + bias_attn).astype(jnp.bfloat16),
            (scaled * gain_mlp + bias_mlp).astype(jnp.bfloat16))


def rotary_split(qkv_all, cos_tab, sin_tab):
    head_dim = qkv_all.shape[-1] // 3
    rot_dim = head_dim // 4
    half_dim = rot_dim // 2
    cos_b = cos_tab[:, None, :]
    sin_b = sin_tab[:, None, :]

    def rotate_vec(vectors):
        rot_part = vectors[..., :rot_dim]
        turned = jnp.concatenate([-rot_part[..., half_dim:], rot_part[..., :half_dim]], axis=-1)
        return jnp.concatenate([rot_part * cos_b + turned * sin_b, vectors[..., rot_dim:]], axis=-1)

    query_rot = rotate_vec(qkv_all[..., :head_dim]).astype(jnp.bfloat16)
    key_rot = rotate_vec(qkv_all[..., head_dim:2 * head_dim]).astype(jnp.bfloat16)
    return query_rot, key_rot, qkv_all[..., 2 * head_dim:].astype(jnp.bfloat16)


def gelu_bf16(pre_act):
    return jax.nn.gelu(pre_act, approximate=False).astype(jnp.bfloat16)


def layer_forward(hidden, weights, cos_tab, sin_tab):
    (ln1_gain, ln1_bias, qkv_weight, qkv_bias, out_weight, out_bias,
     ln2_gain, ln2_bias, up_weight, up_bias, down_weight, down_bias) = weights
    num_heads = qkv_weight.shape[1]
    head_dim = qkv_weight.shape[2] // 3
    d_model = hidden.shape[-1]
    seq_len = hidden.shape[1]
    hidden32 = hidden.astype(jnp.float32)
    (normed_attn, normed_mlp), norm_pull = jax.vjp(
        norm_pair, hidden32, ln1_gain.astype(jnp.float32), ln1_bias.astype(jnp.float32),
        ln2_gain.astype(jnp.float32), ln2_bias.astype(jnp.float32))
    qkv_all = product('bsd,dhe->bshe', normed_attn, qkv_weight) + qkv_bias.astype(jnp.float32).reshape(num_heads, 3 * head_dim)
    (query_rot, key_rot, values), rotary_pull = jax.vjp(
        functools.partial(rotary_split, cos_tab=cos_tab, sin_tab=sin_tab), qkv_all)
    scores = product('bqhd,bkhd->bhqk', query_rot, key_rot) * head_dim ** -0.5
    causal = lax.broadcasted_iota(jnp.int32, (seq_len, seq_len), 0) >= lax.broadcasted_iota(jnp.int32, (seq_len, seq_len), 1)
    attn_probs = jax.nn.softmax(jnp.where(causal, scores, -1e30), axis=-1)
    probs_bf = attn_probs.astype(jnp.bfloat16)
    context = product('bhqk,bkhd->bqhd', probs_bf, values).astype(jnp.bfloat16)
    out_heads = out_weight.reshape(num_heads, head_dim, d_model)
    attn_out = product('bqhd,hde->bqe', context, out_heads) + out_bias.astype(jnp.float32)
    pre_act = product('bsd,df->bsf', normed_mlp, up_weight) + up_bias.astype(jnp.float32)
    mlp_act, gelu_pull = jax.vjp(gelu_bf16, pre_act)
    mlp_out = product('bsf,fd->bsd', mlp_act, down_weight) + down_bias.astype(jnp.float32)
    layer_out = (hidden32 + attn_out + mlp_out).astype(jnp.bfloat16)
    saved_state = (norm_pull, normed_attn, normed_mlp, rotary_pull, query_rot, key_rot, values,
                   attn_probs, probs_bf, context, gelu_pull, mlp_act)
    return layer_out, saved_state


def layer_backward(d_out, weights, saved_state):
    (ln1_gain, ln1_bias, qkv_weight, qkv_bias, out_weight, out_bias,
     ln2_gain, ln2_bias, up_weight, up_bias, down_weight, down_bias) = weights
    (norm_pull, normed_attn, normed_mlp, rotary_pull, query_rot, key_rot, values,
     attn_probs, probs_bf, context, gelu_pull, mlp_act) = saved_state
    num_heads = qkv_weight.shape[1]
    head_dim = qkv_weight.shape[2] // 3
    d_model = d_out.shape[-1]
    d_out32 = d_out.astype(jnp.float32)
    out_sum_grad = jnp.sum(d_out32, axis=(0, 1))
    down_grad = product('bsf,bsd->fd', mlp_act, d_out)
    d_act = product('bsd,fd->bsf', d_out, down_weight).astype(jnp.bfloat16)
    (d_pre,) = gelu_pull(d_act)
    up_bias_grad = jnp.sum(d_pre, axis=(0, 1))
    d_pre_bf = d_pre.astype(jnp.bfloat16)
    up_grad = product('bsd,bsf->df', normed_mlp, d_pre_bf)
    d_normed_mlp = product('bsf,df->bsd', d_pre_bf, up_weight).astype(jnp.bfloat16)
    out_heads = out_weight.reshape(num_heads, head_dim, d_model)
    out_grad = product('bqhd,bqe->hde', context, d_out).reshape(d_model, d_model)
    d_context = product('bqe,hde->bqhd', d_out, out_heads).astype(jnp.bfloat16)
    d_probs = product('bqhd,bkhd->bhqk', d_context, values).astype(jnp.bfloat16).astype(jnp.float32)
    d_values = product('bhqk,bqhd->bkhd', probs_bf, d_context).astype(jnp.bfloat16)
    d_scores = (attn_probs * (d_probs - jnp.sum(d_probs * attn_probs, axis=-1, keepdims=True)) * head_dim ** -0.5).astype(jnp.bfloat16)
    d_query = product('bhqk,bkhd->bqhd', d_scores, key_rot).astype(jnp.bfloat16)
    d_key = product('bhqk,bqhd->bkhd', d_scores, query_rot).astype(jnp.bfloat16)
    (d_qkv,) = rotary_pull((d_query, d_key, d_values))
    qkv_bias_grad = jnp.sum(d_qkv, axis=(0, 1)).reshape(-1)
    d_qkv_bf = d_qkv.astype(jnp.bfloat16)
    qkv_grad = product('bsd,bshe->dhe', normed_attn, d_qkv_bf)
    d_normed_attn = product('bshe,dhe->bsd', d_qkv_bf, qkv_weight).astype(jnp.bfloat16)
    d_hidden32, gain1_grad, bias1_grad, gain2_grad, bias2_grad = norm_pull((d_normed_attn, d_normed_mlp))
    d_hidden = (d_out32 + d_hidden32).astype(jnp.bfloat16)
    grad_list = (gain1_grad, bias1_grad, qkv_grad, qkv_bias_grad, out_grad, out_sum_grad,
                 gain2_grad, bias2_grad, up_grad, up_bias_grad, down_grad, out_sum_grad)
    return d_hidden, grad_list


def solution(mesh):
    shard_axes = ('node', 'local')
    act_spec = P(shard_axes)
    param_spec = P(None, shard_axes)

    def gather_layer(shards, layer_idx):
        return [lax.all_gather(tensor[layer_idx], shard_axes, axis=0, tiled=True) for tensor in shards]

    def scatter_grads(grad_list):
        return [lax.psum_scatter(grad_arr, shard_axes, scatter_dimension=0, tiled=True).astype(jnp.bfloat16)
                for grad_arr in grad_list]

    def device_step(x, y_cot, *shards):
        num_layers = shards[0].shape[0]
        cos_tab, sin_tab = rope_tables(x.shape[1], shards[2].shape[3] // 12)
        layer_inputs = []
        hidden = x
        for layer_idx in range(num_layers):
            layer_inputs.append(hidden)
            hidden, _ = layer_forward(hidden, gather_layer(shards, layer_idx), cos_tab, sin_tab)
        y_out = hidden
        d_hidden = y_cot
        layer_grads = [None] * num_layers
        for layer_idx in reversed(range(num_layers)):
            _, saved_state = layer_forward(layer_inputs[layer_idx], gather_layer(shards, layer_idx), cos_tab, sin_tab)
            d_hidden, grad_list = layer_backward(d_hidden, gather_layer(shards, layer_idx), saved_state)
            layer_grads[layer_idx] = scatter_grads(grad_list)
        stacked = tuple(jnp.stack([layer_grads[i][j] for i in range(num_layers)]) for j in range(len(shards)))
        return (y_out, d_hidden) + stacked

    return jax.shard_map(device_step, mesh=mesh,
                         in_specs=(act_spec, act_spec) + (param_spec,) * 12,
                         out_specs=(act_spec, act_spec) + (param_spec,) * 12,
                         check_vma=False)
```

profile of v0, /device:TPU:0, one launch (start us, length us, event | category | flops | bytes accessed | tf_op | source)
XLA Modules:
  0.0 712.0 jit_solution(16137585359559502324)
XLA Ops:
  7.3 1.8 slice_bitcast_fusion.10
  9.9 1.7 fusion.294
  11.7 1.7 fusion.293
  18.4 35.3 %all-reduce.51 = (bf16[1536]{0:T(1024)(128)(2,1)S(1)}, bf16[1536]{0:T(1024)(128)(2,1)S(1)}, bf16[512]{0:T(512)(128)(2,1)S(1)}, bf16[512]{0:T(512)(128)(2,1)S(1)}...) all-reduce(bf16[1536]{0:T(1024)(128)(2,1)S(1)} %dynamic-update-slic, ...), channel_id=5, replica_groups=mesh['node'=2,'local'=8] {'node','local'}, use_global_device_ids=true, to_apply=%add.24 | all-reduce | flops 9216 | bytes 36864
  54.4 12.5 %all-gather.21 = bf16[1,2048]{1,0:T(2,128)(2,1)S(1)} all-gather(bf16[1,128]{1,0:T(2,128)(2,1)S(1)} %get-tuple-element.133), channel_id=23, replica_groups=mesh['node'=2,'local'=8] {'node','local'}, dimensions={1}, use_global_device_ids=true | all-gather | bytes 4352 | tf_op jit(solution)/shard_map/all_gather | solution.py:122
  68.2 11.5 %all-gather.9 = bf16[1,2048]{1,0:T(2,128)(2,1)S(1)} all-gather(bf16[1,128]{1,0:T(2,128)(2,1)S(1)} %get-tuple-element.134), channel_id=11, replica_groups=mesh['node'=2,'local'=8] {'node','local'}, dimensions={1}, use_global_device_ids=true | all-gather | bytes 4352 | tf_op jit(solution)/shard_map/all_gather | solution.py:122
  80.5 13.5 %all-gather.16 = bf16[1,512,512]{2,1,0:T(8,128)(2,1)S(1)} all-gather(bf16[1,32,512]{2,1,0:T(8,128)(2,1)S(1)} %get-tuple-element.121), channel_id=18, replica_groups=mesh['node'=2,'local'=8] {'node','local'}, dimensions={1}, use_global_device_ids=true | all-gather | bytes 557056 | tf_op jit(solution)/shard_map/all_gather | solution.py:122
  94.0 13.0 %all-gather.4 = bf16[1,512,512]{2,1,0:T(8,128)(2,1)S(1)} all-gather(bf16[1,32,512]{2,1,0:T(8,128)(2,1)S(1)} %get-tuple-element.122), channel_id=6, replica_groups=mesh['node'=2,'local'=8] {'node','local'}, dimensions={1}, use_global_device_ids=true | all-gather | bytes 557056 | tf_op jit(solution)/shard_map/all_gather | solution.py:122
  108.0 3.6 copy.42
  113.0 2.2 fusion.301
  115.2 1.9 convolution_convert_fusion.9
  117.5 3.5 copy.45
  121.0 8.4 %multiply_convert_fusion.1 = (bf16[256,2048]{1,0:T(8,128)(2,1)}, f32[256,2048]{1,0:T(8,128)}, f32[256,2048]{1,0:T(8,128)}) fusion(f32[2048]{0:T(1024)S(1)} %bitcast.425, bf16[1,512,2048]{2,1,0:T(8,128)(2,1)} %all-gather.33.cloned.1.call-done, bf16[1,256,512]{2,1,0:T(8,128)(2,1)S(1)} %copy-done, f32[512]{0:T(512)S(1)} %convert_element_type.550, ...), kind=kOutput, calls=%fused_computation.65 | convolution fusion | flops 572260352 | bytes 7616512 | tf_op jit(solution)/shard_map/bsd,df->bsf/dot_general | solution.py:11
  129.4 6.9 all-gather.35.cloned.1.call-done
  136.3 2.7 fusion.302
  141.9 1.5 convolution_convert_fusion.3
  143.3 3.9 fusion.303
  147.2 3.9 fusion.127
  151.9 4.5 fusion.130
  163.1 2.1 fusion.137
  165.3 3.1 fusion.304
  168.4 8.4 %multiply_convert_fusion = (bf16[256,2048]{1,0:T(8,128)(2,1)S(1)}, f32[256,2048]{1,0:T(8,128)}, f32[256,2048]{1,0:T(8,128)}) fusion(f32[2048]{0:T(1024)S(1)} %bitcast.424, bf16[1,512,2048]{2,1,0:T(8,128)(2,1)} %all-gather.39.cloned.1.call-done, f32[1,256,512]{2,1,0:T(8,128)S(1)} %get-tuple-element.153, f32[512]{0:T(512)S(1)} %convert_element_type.556, ...), kind=kOutput, calls=%fused_computation.50 | convolution fusion | flops 572129280 | bytes 7878656 | tf_op jit(solution)/shard_map/bsd,df->bsf/dot_general | solution.py:11
  176.8 20.3 %all-gather.41.cloned.1.call-done = bf16[1,2048,512]{2,1,0:T(8,128)(2,1)} async-done(((bf16[1,128,512]{2,1,0:T(8,128)(2,1)}), bf16[1,2048,512]{2,1,0:T(8,128)(2,1)}) %all-gather.41.cloned.1.call-update) | async-done | bytes 2097168 | tf_op jit(solution)/shard_map/all_gather | solution.py:122
  197.1 4.9 fusion.306
  202.0 1.4 fusion.173
  204.5 1.3 fusion.195
  205.9 3.8 fusion.188
  211.8 2.5 convolution_convert_fusion.2
  214.3 4.6 fusion.133
  220.0 4.8 fusion.136
  228.7 2.9 fusion.190
  231.7 4.1 fusion.179
  236.1 4.1 fusion.307
  241.2 2.8 fusion.176
  244.1 3.9 fusion.197
  248.1 2.8 fusion.203
  251.8 1.4 fusion.139
  254.4 2.0 fusion.305
  258.5 33.5 %all-reduce.50 = (bf16[512]{0:T(512)(128)(2,1)S(1)}, bf16[512]{0:T(512)(128)(2,1)S(1)}, bf16[512]{0:T(512)(128)(2,1)S(1)}, bf16[512]{0:T(512)(128)(2,1)S(1)}, bf...) all-reduce(f32[512]{0:T(512)S(1)} %copy-done.65, ...), channel_id=27, replica_groups=mesh['node'=2,'local'=8] {'node','local'}, use_global_device_ids=true, to_apply=%region_17.18.clone | all-reduce | flops 12288 | bytes 73728
  296.2 1.3 fusion.287
  299.5 1.4 fusion.91
  301.8 9.3 %reduce-scatter.13.cloned.1.call-done = f32[32,512]{1,0:T(8,128)} async-done(((f32[512,512]{1,0:T(8,128)}), f32[32,512]{1,0:T(8,128)}) %reduce-scatter.13.cloned.1.call-update) | async-done | bytes 65552 | tf_op jit(solution)/shard_map/reduce_scatter | solution.py:125
  312.5 62.9 %reduce-scatter.11.cloned.1.call-done = f32[32,8,192]{2,0,1:T(8,128)} async-done(((f32[512,8,192]{2,0,1:T(8,128)}), f32[32,8,192]{2,0,1:T(8,128)}) %reduce-scatter.11.cloned.1.call-update) | async-done | bytes 196624 | tf_op jit(solution)/shard_map/reduce_scatter | solution.py:125
  376.4 64.4 %reduce-scatter.9.cloned.1.call-done = f32[32,8,192]{2,0,1:T(8,128)} async-done(((f32[512,8,192]{2,0,1:T(8,128)}), f32[32,8,192]{2,0,1:T(8,128)}) %reduce-scatter.9.cloned.1.call-update) | async-done | bytes 196624 | tf_op jit(solution)/shard_map/reduce_scatter | solution.py:125
  442.7 63.9 %reduce-scatter.19.cloned.1.call-done = f32[32,2048]{1,0:T(8,128)} async-done(((f32[512,2048]{1,0:T(8,128)}), f32[32,2048]{1,0:T(8,128)}) %reduce-scatter.19.cloned.1.call-update) | async-done | bytes 262160 | tf_op jit(solution)/shard_map/reduce_scatter | solution.py:125
  507.5 64.4 %reduce-scatter.17.cloned.1.call-done = f32[32,2048]{1,0:T(8,128)} async-done(((f32[512,2048]{1,0:T(8,128)}), f32[32,2048]{1,0:T(8,128)}) %reduce-scatter.17.cloned.1.call-update) | async-done | bytes 262160 | tf_op jit(solution)/shard_map/reduce_scatter | solution.py:125
  573.6 63.8 %reduce-scatter.21.cloned.1.call-done = f32[128,512]{1,0:T(8,128)} async-done(((f32[2048,512]{1,0:T(8,128)}), f32[128,512]{1,0:T(8,128)}) %reduce-scatter.21.cloned.1.call-update) | async-done | bytes 262160 | tf_op jit(solution)/shard_map/reduce_scatter | solution.py:125
  638.4 64.4 %reduce-scatter.23.cloned.1.call-done = f32[128,512]{1,0:T(8,128)} async-done(((f32[2048,512]{1,0:T(8,128)}), f32[128,512]{1,0:T(8,128)}) %reduce-scatter.23.cloned.1.call-update) | async-done | bytes 262160 | tf_op jit(solution)/shard_map/reduce_scatter | solution.py:125
  (334 shorter events, 52.0 us)
Async XLA Ops:
  7.2 7.5 %copy-start = (bf16[1,256,512]{2,1,0:T(8,128)(2,1)S(1)}, bf16[1,256,512]{2,1,0:T(8,128)(2,1)}, u32[]{:S(2)}) copy-start(bf16[1,256,512]{2,1,0:T(8,128)(2,1)} %param.14) | copy-start | bytes 786436
  7.2 7.9 %copy-start.55 = (bf16[2,32]{1,0:T(2,128)(2,1)S(1)}, bf16[2,32]{1,0:T(2,128)(2,1)}, u32[]{:S(2)}) copy-start(bf16[2,32]{1,0:T(2,128)(2,1)} %param.16) | copy-start | bytes 388
  7.2 7.9 %copy-start.56 = (bf16[2,32]{1,0:T(2,128)(2,1)S(1)}, bf16[2,32]{1,0:T(2,128)(2,1)}, u32[]{:S(2)}) copy-start(bf16[2,32]{1,0:T(2,128)(2,1)} %param.17) | copy-start | bytes 388
  7.2 7.9 %copy-start.57 = (bf16[2,96]{1,0:T(2,128)(2,1)S(1)}, bf16[2,96]{1,0:T(2,128)(2,1)}, u32[]{:S(2)}) copy-start(bf16[2,96]{1,0:T(2,128)(2,1)} %param.19) | copy-start | bytes 1156
  7.2 7.9 %copy-start.58 = (bf16[2,32]{1,0:T(2,128)(2,1)S(1)}, bf16[2,32]{1,0:T(2,128)(2,1)}, u32[]{:S(2)}) copy-start(bf16[2,32]{1,0:T(2,128)(2,1)} %param.21) | copy-start | bytes 388
  7.2 7.9 %copy-start.59 = (bf16[2,32]{1,0:T(2,128)(2,1)S(1)}, bf16[2,32]{1,0:T(2,128)(2,1)}, u32[]{:S(2)}) copy-start(bf16[2,32]{1,0:T(2,128)(2,1)} %param.22) | copy-start | bytes 388
  7.2 7.9 %copy-start.60 = (bf16[2,32]{1,0:T(2,128)(2,1)S(1)}, bf16[2,32]{1,0:T(2,128)(2,1)}, u32[]{:S(2)}) copy-start(bf16[2,32]{1,0:T(2,128)(2,1)} %param.23) | copy-start | bytes 388
  7.3 7.9 %copy-start.61 = (bf16[2,128]{1,0:T(2,128)(2,1)S(1)}, bf16[2,128]{1,0:T(2,128)(2,1)}, u32[]{:S(2)}) copy-start(bf16[2,128]{1,0:T(2,128)(2,1)} %param.25) | copy-start | bytes 1540
  7.3 8.0 %copy-start.62 = (bf16[2,32]{1,0:T(2,128)(2,1)S(1)}, bf16[2,32]{1,0:T(2,128)(2,1)}, u32[]{:S(2)}) copy-start(bf16[2,32]{1,0:T(2,128)(2,1)} %param.27) | copy-start | bytes 388
  7.3 73.2 %copy-start.38 = (bf16[2,32,512]{2,1,0:T(8,128)(2,1)S(1)}, bf16[2,32,512]{2,1,0:T(8,128)(2,1)}, u32[]{:S(2)}) copy-start(bf16[2,32,512]{2,1,0:T(8,128)(2,1)} %param.20) | copy-start | bytes 196612
  7.3 100.8 %all-gather.31.cloned.1.call-start = ((), (), s32[]{:S(2)}) async-start(), calls=%async_computation.16 | async-start | bytes 2228224 | tf_op jit(solution)/shard_map/all_gather | solution.py:122
  9.1 97.9 %copy-start.8 = (bf16[1,256,512]{2,1,0:T(8,128)(2,1)S(1)}, bf16[1,256,512]{2,1,0:T(8,128)(2,1)}, u32[]{:S(2)}) copy-start(bf16[1,256,512]{2,1,0:T(8,128)(2,1)} %param.15) | copy-start | bytes 786436
  9.1 108.4 %all-gather.37.cloned.1.call-start = ((), (), s32[]{:S(2)}) async-start(), calls=%async_computation.19 | async-start | bytes 2228224 | tf_op jit(solution)/shard_map/all_gather | solution.py:122
  9.9 111.1 %all-gather.33.cloned.1.call-start = ((), (), s32[]{:S(2)}) async-start(), calls=%async_computation.17 | async-start | bytes 2228224 | tf_op jit(solution)/shard_map/all_gather | solution.py:122
  11.6 124.6 %all-gather.35.cloned.1.call-start = ((), (), s32[]{:S(2)}) async-start(), calls=%async_computation.18 | async-start | bytes 2228224 | tf_op jit(solution)/shard_map/all_gather | solution.py:122
  13.4 155.0 %all-gather.39.cloned.1.call-start = ((), (), s32[]{:S(2)}) async-start(), calls=%async_computation.20 | async-start | bytes 2228224 | tf_op jit(solution)/shard_map/all_gather | solution.py:122
  14.0 183.1 %all-gather.41.cloned.1.call-start = ((), (), s32[]{:S(2)}) async-start(), calls=%async_computation.21 | async-start | bytes 2228224 | tf_op jit(solution)/shard_map/all_gather | solution.py:122
  14.6 286.4 %reduce-scatter.15.cloned.1.call-start = ((), (), s32[]{:S(2)}) async-start(), calls=%async_computation.11 | async-start | bytes 1114112 | tf_op jit(solution)/shard_map/reduce_scatter | solution.py:125
  15.0 3.1 copy-start.46
  94.0 13.0 %copy-start.13 = (bf16[1,512,512]{2,1,0:T(8,128)(2,1)}, bf16[1,512,512]{2,1,0:T(8,128)(2,1)S(1)}, u32[]{:S(2)}) copy-start(bf16[1,512,512]{2,1,0:T(8,128)(2,1)S(1)} %all-gather.16) | copy-start | bytes 1572868
  107.0 10.1 %copy-start.15 = (bf16[1,512,512]{2,1,0:T(8,128)(2,1)}, bf16[1,512,512]{2,1,0:T(8,128)(2,1)S(1)}, u32[]{:S(2)}) copy-start(bf16[1,512,512]{2,1,0:T(8,128)(2,1)S(1)} %all-gather.4) | copy-start | bytes 1572868
  117.1 3.9 copy-start.33
  117.5 3.6 copy-start.53
  140.2 7.0 copy-start.12
  147.2 4.7 copy-start.37
  147.2 4.7 copy-start.43
  147.2 4.7 copy-start.77
  156.5 3.2 copy-start.18
  165.2 3.2 copy-start.22
  165.2 3.1 copy-start.52
  165.3 145.8 %reduce-scatter.13.cloned.1.call-start = ((), (), s32[]{:S(2)}) async-start(), calls=%async_computation.10 | async-start | bytes 1114112 | tf_op jit(solution)/shard_map/reduce_scatter | solution.py:125
  176.8 71.3 %copy-start.9 = (bf16[256,2048]{1,0:T(8,128)(2,1)}, bf16[256,2048]{1,0:T(8,128)(2,1)S(1)}, u32[]{:S(2)}) copy-start(bf16[256,2048]{1,0:T(8,128)(2,1)S(1)} %get-tuple-element.82) | copy-start | bytes 3145732
  197.1 4.9 copy-start.30
  197.1 4.9 copy-start.70
  205.9 169.6 %reduce-scatter.11.cloned.1.call-start = ((), (), s32[]{:S(2)}) async-start(), calls=%async_computation.9 | async-start | bytes 4456448 | tf_op jit(solution)/shard_map/reduce_scatter | solution.py:125
  209.7 4.5 copy-start.42
  209.8 231.1 %reduce-scatter.9.cloned.1.call-start = ((), (), s32[]{:S(2)}) async-start(), calls=%async_computation.8 | async-start | bytes 4456448 | tf_op jit(solution)/shard_map/reduce_scatter | solution.py:125
  214.3 5.7 copy-start.40
  214.3 5.7 copy-start.75
  231.6 274.9 %reduce-scatter.19.cloned.1.call-start = ((), (), s32[]{:S(2)}) async-start(), calls=%async_computation.13 | async-start | bytes 4456448 | tf_op jit(solution)/shard_map/reduce_scatter | solution.py:125
  235.8 336.1 %reduce-scatter.17.cloned.1.call-start = ((), (), s32[]{:S(2)}) async-start(), calls=%async_computation.12 | async-start | bytes 4456448 | tf_op jit(solution)/shard_map/reduce_scatter | solution.py:125
  244.0 393.4 %reduce-scatter.21.cloned.1.call-start = ((), (), s32[]{:S(2)}) async-start(), calls=%async_computation.14 | async-start | bytes 4456448 | tf_op jit(solution)/shard_map/reduce_scatter | solution.py:125
  248.0 454.8 %reduce-scatter.23.cloned.1.call-start = ((), (), s32[]{:S(2)}) async-start(), calls=%async_computation.15 | async-start | bytes 4456448 | tf_op jit(solution)/shard_map/reduce_scatter | solution.py:125
  250.9 3.5 copy-start.2
  256.8 39.4 %copy-start.47 = (f32[256]{0:T(256)S(1)}, f32[256]{0:T(256)}, u32[]{:S(2)}) copy-start(f32[256]{0:T(256)} %copy-done.46) | copy-start | bytes 3076
  258.0 40.4 %copy-start.14 = (bf16[1,512,512]{2,1,0:T(8,128)(2,1)S(1)}, bf16[1,512,512]{2,1,0:T(8,128)(2,1)}, u32[]{:S(2)}) copy-start(bf16[1,512,512]{2,1,0:T(8,128)(2,1)} %copy-done.13) | copy-start | bytes 1572868
  258.3 40.0 %copy-start.32 = (bf16[8,64,256]{2,1,0:T(8,128)(2,1)S(1)}, bf16[8,64,256]{2,1,0:T(8,128)(2,1)}, u32[]{:S(2)}) copy-start(bf16[8,64,256]{2,1,0:T(8,128)(2,1)} %copy-done.31) | copy-start | bytes 786436
  292.1 412.4 %copy-start.71 = (bf16[2,32]{1,0:T(2,128)(2,1)}, bf16[2,32]{1,0:T(2,128)(2,1)S(1)}, u32[]{:S(2)}) copy-start(bf16[2,32]{1,0:T(2,128)(2,1)S(1)} %pad_maximum_fusion.32) | copy-start | bytes 388
  (45 other events, 69.6 us)
Sparse Core Ops, SparseCore 0:
  10.9 31.4 all-gather.30
  45.2 28.3 all-gather.36
  75.9 29.7 all-gather.32
  107.7 28.4 all-gather.34
  138.4 28.2 all-gather.38
  168.8 28.2 all-gather.40
  199.3 55.3 reduce-scatter.14
  257.0 54.0 reduce-scatter.12
  313.3 62.0 reduce-scatter.10
  377.6 63.2 reduce-scatter.8
  443.1 63.4 reduce-scatter.18
  508.7 63.1 reduce-scatter.16
  574.2 63.2 reduce-scatter.20
  639.6 63.2 reduce-scatter.22
where the time goes:
time: 720 us; the launch traced here: 712 us
  waiting for transfers between devices  422 us (59%)
  blocking collectives  119 us (17%)
  matrix products  97.3 us (14%)
  local copies, waits for them, and re-layouts  29.4 us (4%)
  other arithmetic  27.4 us (4%)
  between operations  15.6 us (2%)
    reduce_scatter x8, waiting for transfers between devices, scatter_grads(): lax.psum_scatter(grad_arr, shard_axes, scatter_dimension=0, tiled=True)  393 us
    dot_general x32, matrix products, product(): jnp.einsum(einsum_form, first_op, second_op, preferred_element_type=jnp.f...  89.8 us
    unnamed x2, blocking collectives  68.7 us
    all_gather x4, blocking collectives, gather_layer(): lax.all_gather(tensor[layer_idx], shard_axes, axis=0, tiled=True)  50.6 us
    all_gather x6, waiting for transfers between devices, gather_layer(): lax.all_gather(tensor[layer_idx], shard_axes, axis=0, tiled=True)  27.2 us
  transfers between devices with their start and end apart: 14, of which 9 were waited for; matrix products, arithmetic and copies ran while one was open for 20% of the time, Pallas kernels for 0%

commit v1 on v0

v1 whole, which is shorter than its diff:
```python
import numpy as np
import jax
import jax.numpy as jnp
from jax import lax
from jax.experimental import pallas as pl
from jax.experimental.pallas import tpu as pltpu
from jax.sharding import PartitionSpec as P

BF, F32 = jnp.bfloat16, jnp.float32
MESH = pl.DeviceIdType.MESH
EPSILON = 1e-5
LAYERS, SEQ, DM, FF, ND = 2, 256, 512, 2048, 16
SH, HD, LN, Q3 = 32, 64, 128, 1536
ROWS = (SH, SH, LN)
COLS = (FF, FF, DM)
AO, UP, DN = 0, 1, 2
ORDERS = ((1, 2, 4), (2, 4, 1), (4, 1, 2))


def bit(v, a):
    return lax.rem(lax.div(v, a), 2)


def flip(v, mask):
    for a in (1, 2, 4):
        if mask & a:
            v = v + a - 2 * a * bit(v, a)
    return v


def mm(a, b):
    return jnp.dot(a, b, preferred_element_type=F32)


def mm_nt(a, b):
    return lax.dot_general(a, b, (((1,), (1,)), ((), ())), preferred_element_type=F32)


def mm_tn(a, b):
    return lax.dot_general(a, b, (((0,), (0,)), ((), ())), preferred_element_type=F32)


def axis_of(a, axes):
    return axes.index(a)


def kernel(x_ref, cot_ref, wa_in, wu_in, wd_in, small_in, rc_ref, r1_ref, r2_ref,
           y_ref, xg_ref, oa_ref, ou_ref, od_ref, os_ref,
           wa, wu, wd, ga, gu, gd, ra0, ru0, rd0, ra1, ru1, rd1, ra2, ru2, rd2, ra3, ru3, rd3,
           smalls, vec, upb, qkvb, gs, gr, gvec, gub, gqb,
           h1, dh, na, nm, nat, nmt, qkv, dqkv, ctx, dctx, acc, dnm,
           loc_sem, ag_send, ag_ici, ag_d2d, rs_send, rs_recv, sm_send, sm_recv, gr_send, gr_recv):
    me = lax.axis_index('node') * 8 + lax.axis_index('local')
    chip = lax.div(me, 2)
    core = lax.rem(me, 2)
    other = 1 - core
    W, G = (wa, wu, wd), (ga, gu, gd)
    R0, R1, R2, R3 = (ra0, ru0, rd0), (ra1, ru1, rd1), (ra2, ru2, rd2), (ra3, ru3, rd3)
    pend = []

    def dev(c, k):
        i = c * 2 + k
        return (lax.div(i, 8), lax.rem(i, 8))

    def block(l, w, c, k):
        return W[w].at[l, pl.ds(pl.multiple_of((c * 2 + k) * ROWS[w], ROWS[w]), ROWS[w])]

    counts = {}

    def ag_copy(l, w, src_mask, to, recv_sem):
        n = counts.get((l, w), 0)
        counts[(l, w)] = n + 1
        blk = block(l, w, flip(chip, src_mask), core)
        cp = pltpu.make_async_remote_copy(src_ref=blk, dst_ref=blk, send_sem=ag_send.at[l, w, n],
                                          recv_sem=recv_sem, device_id=to, device_id_type=MESH)
        cp.start()
        pend.append(cp)

    def to_link(l, w, mask, a):
        ag_copy(l, w, mask, dev(flip(chip, a), core), ag_ici.at[l, w, mask ^ a])

    def to_partner(l, w, mask):
        ag_copy(l, w, mask, dev(chip, other), ag_d2d.at[l, w, mask])

    def got(l, w, mask):
        blk = block(l, w, flip(chip, mask), core)
        pltpu.make_async_remote_copy(src_ref=blk, dst_ref=blk, send_sem=ag_send.at[l, w, 0],
                                     recv_sem=ag_ici.at[l, w, mask], device_id=dev(flip(chip, 1), core),
                                     device_id_type=MESH).wait_recv()

    def got_partner(l, w):
        for mask in range(8):
            blk = block(l, w, flip(chip, mask), other)
            pltpu.make_async_remote_copy(src_ref=blk, dst_ref=blk, send_sem=ag_send.at[l, w, 0],
                                         recv_sem=ag_d2d.at[l, w, mask], device_id=dev(chip, other),
                                         device_id_type=MESH).wait_recv()

    def ag0(l, w):
        a, b, c = ORDERS[w]
        to_link(l, w, 0, a)
        to_link(l, w, 0, b)
        to_link(l, w, 0, c)
        to_partner(l, w, 0)

    def ag1(l, w):
        a, b, c = ORDERS[w]
        got(l, w, a)
        to_link(l, w, a, b)
        to_link(l, w, a, c)
        to_partner(l, w, a)

    def ag2(l, w):
        a, b, c = ORDERS[w]
        for m in (b, a | b):
            got(l, w, m)
            to_link(l, w, m, c)
            to_partner(l, w, m)

    def ag3(l, w):
        a, b, c = ORDERS[w]
        for m in (c, a | c, b | c, 7):
            got(l, w, m)
            to_partner(l, w, m)

    def rs_copy(l, w, stage, src, dst, to):
        cp = pltpu.make_async_remote_copy(src_ref=src, dst_ref=dst, send_sem=rs_send.at[l, w, stage],
                                          recv_sem=rs_recv.at[l, w, stage], device_id=to, device_id_type=MESH)
        cp.start()
        return cp

    rs = {}

    def s0(l, w):
        rs[l, w, 0] = rs_copy(l, w, 0, G[w].at[:, :, :, other], R0[w].at[l], dev(chip, other))

    def pick(ax, n, v):
        return tuple(v if i == ax else slice(None) for i in range(n))

    def s1(l, w):
        a, b, c = ORDERS[w]
        rs[l, w, 0].wait_recv()
        for z in range(2):
            for y in range(2):
                for x in range(2):
                    R0[w][l, z, y, x] = R0[w][l, z, y, x] + G[w][z, y, x, core]
        ax = axis_of(a, [4, 2, 1])
        rs[l, w, 1] = rs_copy(l, w, 1, R0[w].at[(l,) + pick(ax, 3, 1 - bit(chip, a))], R1[w].at[l],
                              dev(flip(chip, a), core))

    def s2(l, w):
        a, b, c = ORDERS[w]
        rs[l, w, 1].wait_recv()
        ax = axis_of(a, [4, 2, 1])
        mine = bit(chip, a)
        for i in range(2):
            for j in range(2):
                idx = [i, j]
                idx.insert(ax, mine)
                R1[w][l, i, j] = R1[w][l, i, j] + R0[w][(l,) + tuple(idx)]
        ax = axis_of(b, [m for m in (4, 2, 1) if m != a])
        rs[l, w, 2] = rs_copy(l, w, 2, R1[w].at[(l,) + pick(ax, 2, 1 - bit(chip, b))], R2[w].at[l],
                              dev(flip(chip, b), core))

    def s3(l, w):
        a, b, c = ORDERS[w]
        rs[l, w, 2].wait_recv()
        ax = axis_of(b, [m for m in (4, 2, 1) if m != a])
        mine = bit(chip, b)
        for i in range(2):
            idx = [i]
            idx.insert(ax, mine)
            R2[w][l, i] = R2[w][l, i] + R1[w][(l,) + tuple(idx)]
        rs[l, w, 3] = rs_copy(l, w, 3, R2[w].at[l, 1 - bit(chip, c)], R3[w].at[l], dev(flip(chip, c), core))

    def s4(l, w):
        c = ORDERS[w][2]
        rs[l, w, 3].wait_recv()
        (oa_ref, ou_ref, od_ref)[w][l] = (R3[w][l] + R2[w][l, bit(chip, c)]).astype(BF)

    def normed(h_bf, l):
        h32 = h_bf.astype(F32)
        cen = h32 - jnp.mean(h32, axis=-1, keepdims=True)
        rstd = lax.rsqrt(jnp.mean(cen * cen, axis=-1, keepdims=True) + EPSILON)
        return cen * rstd, rstd

    def norms(h_ref, l, bwd):
        xhat, _ = normed(h_ref[...], l)
        n1 = (xhat * vec[l, 0:1, :] + vec[l, 1:2, :]).astype(BF)
        n2 = (xhat * vec[l, 3:4, :] + vec[l, 4:5, :]).astype(BF)
        na[...] = n1
        nm[...] = n2
        if bwd:
            nat[...] = n1.T
            nmt[...] = n2.T

    def rope(xs, back):
        c, p, q = rc_ref[...], r1_ref[...], r2_ref[...]
        if back:
            return xs * c + pltpu.roll(xs * p, 8, 1) + pltpu.roll(xs * q, 120, 1)
        return xs * c + pltpu.roll(xs, 120, 1) * p + pltpu.roll(xs, 8, 1) * q

    def make_qkv(l):
        for t in range(3):
            cols = slice(DM * t, DM * t + DM)
            raw = mm(na[...], wa[l, :, cols]) + qkvb[l, :, cols]
            for s in range(4):
                part = raw[:, LN * s:LN * s + LN]
                if t < 2:
                    part = rope(part, False)
                qkv[:, DM * t + LN * s:DM * t + LN * s + LN] = part.astype(BF)

    def heads(l, bwd):
        lane = lax.broadcasted_iota(jnp.int32, (1, LN), 1)
        masks = [(lane < HD).astype(F32).astype(BF), (lane >= HD).astype(F32).astype(BF)]
        causal = (lax.broadcasted_iota(jnp.int32, (SEQ, SEQ), 0) >= lax.broadcasted_iota(jnp.int32, (SEQ, SEQ), 1))

        def body(j, carry):
            col = pl.multiple_of(j * LN, LN)
            q, k, v = (qkv[:, pl.ds(col + DM * t, LN)] for t in range(3))
            ctx_sum = jnp.zeros((SEQ, LN), F32)
            if bwd:
                dc = dctx[:, pl.ds(col, LN)]
                dq = jnp.zeros((SEQ, LN), F32)
                dk = jnp.zeros((SEQ, LN), F32)
                dv = jnp.zeros((SEQ, LN), F32)
            for mask in masks:
                qm = q * mask
                sc = jnp.where(causal, mm_nt(qm, k) * 0.125, -1e30)
                e = jnp.exp(sc - jnp.max(sc, axis=-1, keepdims=True))
                p = e / jnp.sum(e, axis=-1, keepdims=True)
                pb = p.astype(BF)
                ctx_sum = ctx_sum + mm(pb, v * mask)
                if bwd:
                    dcm = dc * mask
                    dp = mm_nt(dcm, v).astype(BF).astype(F32)
                    dv = dv + mm_tn(pb, dcm)
                    ds = (p * (dp - jnp.sum(dp * p, axis=-1, keepdims=True)) * 0.125).astype(BF)
                    dq = dq + mm(ds, k * mask)
                    dk = dk + mm_tn(ds, qm)
            ctx[:, pl.ds(col, LN)] = ctx_sum.astype(BF)
            if bwd:
                for t, d in enumerate((dq, dk, dv)):
                    d = d.astype(BF).astype(F32)
                    if t < 2:
                        d = rope(d, True)
                    gqb[0:1, pl.ds(col + DM * t, LN)] = jnp.sum(d, axis=0, keepdims=True)
                    dqkv[:, pl.ds(col + DM * t, LN)] = d.astype(BF)
            return carry

        lax.fori_loop(0, 4, body, 0)

    def mlp(l, dout, fwd):
        if fwd:
            acc[...] = jnp.zeros_like(acc)
        if dout is not None:
            dnm[...] = jnp.zeros_like(dnm)

        def body(t, carry):
            col = pl.multiple_of(t * DM, DM)
            wu_t = wu[l, :, pl.ds(col, DM)]
            wd_t = wd[l, pl.ds(col, DM), :]
            pre = mm(nm[...], wu_t) + upb[l, :, pl.ds(col, DM)]
            cdf = 0.5 * (1.0 + lax.erf(pre * 0.7071067811865476))
            act = (pre * cdf).astype(BF)
            if fwd:
                acc[...] += mm(act, wd_t)
            if dout is not None:
                slope = cdf + pre * (0.3989422804014327 * jnp.exp(-0.5 * pre * pre))
                gt = mm_tn(act, dout[...])
                t4 = lax.div(t, 2)
                for i in range(2):
                    gd[t4, lax.rem(t, 2), i] = gt[256 * i:256 * i + 256].reshape(2, LN, DM)
                dpre = mm_nt(dout[...], wd_t).astype(BF).astype(F32) * slope
                gub[0:1, pl.ds(col, DM)] = jnp.sum(dpre, axis=0, keepdims=True)
                dpb = dpre.astype(BF)
                gu[:, :, :, :, :, pl.ds(col, DM)] = mm(nmt[...], dpb).reshape(2, 2, 2, 2, SH, DM)
                dnm[...] += mm_nt(dpb, wu_t)
            return carry

        lax.fori_loop(0, 4, body, 0)

    def attn_grads(l, dout):
        ga[:, :, :, :, :, Q3:FF] = mm_tn(ctx[...], dout[...]).reshape(2, 2, 2, 2, SH, DM)
        for t in range(3):
            cols = slice(DM * t, DM * t + DM)
            ga[:, :, :, :, :, cols] = mm(nat[...], dqkv[:, cols]).reshape(2, 2, 2, 2, SH, DM)

    def layer_end(h_ref, l, dout):
        dna = mm_nt(dqkv[...], wa[l, :, 0:Q3]).astype(BF).astype(F32)
        dnm32 = dnm[...].astype(BF).astype(F32)
        xhat, rstd = normed(h_ref[...], l)
        d32 = dout[...].astype(F32)
        gvec[0:1, :] = jnp.sum(dna * xhat, axis=0, keepdims=True)
        gvec[1:2, :] = jnp.sum(dna, axis=0, keepdims=True)
        gvec[2:3, :] = jnp.sum(d32, axis=0, keepdims=True)
        gvec[3:4, :] = jnp.sum(dnm32 * xhat, axis=0, keepdims=True)
        gvec[4:5, :] = jnp.sum(dnm32, axis=0, keepdims=True)
        gvec[5:6, :] = gvec[2:3, :]
        dx = dna * vec[l, 0:1, :] + dnm32 * vec[l, 3:4, :]
        dhid = rstd * (dx - jnp.mean(dx, axis=-1, keepdims=True) - xhat * jnp.mean(dx * xhat, axis=-1, keepdims=True))
        return (d32 + dhid).astype(BF)

    def small_grads(l):
        for d in range(ND):
            gs[l, d] = jnp.zeros((8, LN), F32)
            gs[l, d, 0:6, 0:SH] = gvec[0:6, SH * d:SH * d + SH]
            gs[l, d, 6:7, :] = gub[0:1, LN * d:LN * d + LN]
            for lo, col, n in bias_parts(d):
                gs[l, d, 7:8, lo:lo + n] = gqb[0:1, col:col + n]

    def bias_parts(d):
        base = HD * (d // 2)
        if d % 2 == 0:
            return ((0, base, HD), (HD, DM + base, SH))
        return ((0, DM + base + SH, SH), (SH, 1024 + base, HD))

    def peer(i):
        t = lax.rem(me + i, ND)
        return t, (lax.div(t, 8), lax.rem(t, 8))

    def small_send(l):
        def body(i, carry):
            t, to = peer(i)
            pltpu.make_async_remote_copy(src_ref=gs.at[l, t], dst_ref=gr.at[l, me], send_sem=gr_send.at[l],
                                         recv_sem=gr_recv.at[l], device_id=to, device_id_type=MESH).start()
            return carry
        lax.fori_loop(1, ND, body, 0)
        gr[l, me] = gs[l, me]

    def small_finish(l):
        whole = pltpu.make_async_remote_copy(src_ref=gs.at[l, pl.ds(0, ND - 1)], dst_ref=gr.at[l, pl.ds(0, ND - 1)],
                                             send_sem=gr_send.at[l], recv_sem=gr_recv.at[l],
                                             device_id=dev(chip, other), device_id_type=MESH)
        whole.wait_send()
        whole.wait_recv()
        total = gr[l, 0]
        for d in range(1, ND):
            total = total + gr[l, d]
        os_ref[l] = total

    local = []
    for w, src in enumerate((wa_in, wu_in, wd_in)):
        for l in range(LAYERS):
            cp = pltpu.make_async_copy(src.at[l], block(l, w, chip, core), loc_sem.at[l, w])
            cp.start()
            local.append(cp)
    cp = pltpu.make_async_copy(small_in, smalls.at[me], loc_sem.at[0, 3])
    cp.start()
    local.append(cp)
    for cp in local:
        cp.wait()

    def send_small(i, carry):
        t, to = peer(i)
        pltpu.make_async_remote_copy(src_ref=smalls.at[me], dst_ref=smalls.at[me], send_sem=sm_send,
                                     recv_sem=sm_recv, device_id=to, device_id_type=MESH).start()
        return carry

    groups = (AO, UP, DN)
    for w in groups:
        ag0(0, w)
    lax.fori_loop(1, ND, send_small, 0)
    for w in groups:
        ag1(0, w)
    whole = pltpu.make_async_remote_copy(src_ref=smalls.at[pl.ds(0, ND - 1)], dst_ref=smalls.at[pl.ds(0, ND - 1)],
                                         send_sem=sm_send, recv_sem=sm_recv, device_id=dev(chip, other),
                                         device_id_type=MESH)
    whole.wait_send()
    whole.wait_recv()
    for l in range(LAYERS):
        for d in range(ND):
            vec[l, 0:6, SH * d:SH * d + SH] = smalls[d, l, 0:6, 0:SH]
            upb[l, 0:1, LN * d:LN * d + LN] = smalls[d, l, 6:7, :]
            for lo, col, n in bias_parts(d):
                qkvb[l, 0:1, col:col + n] = smalls[d, l, 7:8, lo:lo + n]
    norms(x_ref, 0, False)
    for w in groups:
        ag2(0, w)
    for w in groups:
        ag0(1, w)
    for w in groups:
        ag3(0, w)
    for w in groups:
        ag1(1, w)
    got_partner(0, AO)
    make_qkv(0)
    heads(0, False)
    for w in groups:
        ag2(1, w)
    got_partner(0, UP)
    got_partner(0, DN)
    mlp(0, None, True)
    acc[...] += mm(ctx[...], wa[0, :, Q3:FF])
    h1[...] = (x_ref[...].astype(F32) + acc[...] + vec[0, 2:3, :] + vec[0, 5:6, :]).astype(BF)

    norms(h1, 1, True)
    ag3(1, UP)
    ag3(1, DN)
    got_partner(1, UP)
    got_partner(1, DN)
    mlp(1, cot_ref, True)
    s0(1, DN)
    s0(1, UP)
    ag3(1, AO)
    got_partner(1, AO)
    make_qkv(1)
    dctx[...] = mm_nt(cot_ref[...], wa[1, :, Q3:FF]).astype(BF)
    s1(1, DN)
    s1(1, UP)
    heads(1, True)
    attn_grads(1, cot_ref)
    s0(1, AO)
    acc[...] += mm(ctx[...], wa[1, :, Q3:FF])
    y_ref[...] = (h1[...].astype(F32) + acc[...] + vec[1, 2:3, :] + vec[1, 5:6, :]).astype(BF)
    dh[...] = layer_end(h1, 1, cot_ref)
    small_grads(1)
    small_send(1)
    s1(1, AO)

    norms(x_ref, 0, True)
    rs[1, DN, 0].wait_send()
    rs[1, UP, 0].wait_send()
    mlp(0, dh, False)
    s0(0, DN)
    s0(0, UP)
    make_qkv(0)
    dctx[...] = mm_nt(dh[...], wa[0, :, Q3:FF]).astype(BF)
    s1(0, DN)
    s1(0, UP)
    heads(0, True)
    rs[1, AO, 0].wait_send()
    attn_grads(0, dh)
    s0(0, AO)
    xg_ref[...] = layer_end(x_ref, 0, dh)
    small_grads(0)
    small_send(0)
    s1(0, AO)
    order = ((1, DN), (1, UP), (1, AO), (0, DN), (0, UP), (0, AO))
    for l, w in order:
        s2(l, w)
    for l, w in order:
        s3(l, w)
    for l, w in order:
        s4(l, w)
    small_finish(1)
    small_finish(0)
    for w in groups:
        rs[0, w, 0].wait_send()
        for l in range(LAYERS):
            for stage in range(1, 4):
                rs[l, w, stage].wait_send()
    for cp in pend:
        cp.wait_send()


def rope_constants():
    rot, half, hd = 16, 8, HD
    inv = (1.0 / (10000.0 ** (np.arange(0, rot, 2, dtype=np.float32) / np.float32(rot)))).astype(np.float32)
    ang = np.arange(SEQ, dtype=np.float32)[:, None] * inv[None, :]
    cos, sin = np.cos(ang).astype(np.float32), np.sin(ang).astype(np.float32)
    c = np.ones((SEQ, LN), np.float32)
    p = np.zeros((SEQ, LN), np.float32)
    q = np.zeros((SEQ, LN), np.float32)
    for base in (0, hd):
        c[:, base:base + half] = cos
        c[:, base + half:base + rot] = cos
        p[:, base:base + half] = -sin
        q[:, base + half:base + rot] = sin
    return c, p, q


def solution(mesh):
    shard_axes = ('node', 'local')
    act_spec = P(shard_axes)
    param_spec = P(None, shard_axes)
    consts = rope_constants()
    vm = pl.BlockSpec(memory_space=pltpu.VMEM)
    hbm = pl.BlockSpec(memory_space=pl.ANY)

    def device_step(x, y_cot, g1, b1, wqkv, bqkv, wout, bout, g2, b2, wup, bup, wdn, bdn):
        qkv_cols = wqkv.reshape(LAYERS, SH, 8, 3, HD).transpose(0, 1, 3, 2, 4).reshape(LAYERS, SH, Q3)
        wa = jnp.concatenate([qkv_cols, wout], axis=-1)
        small = jnp.stack([jnp.pad(v, ((0, 0), (0, LN - v.shape[1])))
                           for v in (g1, b1, bout, g2, b2, bdn, bup, bqkv)], axis=1).astype(F32)

        def v(shape, dt):
            return pltpu.VMEM(shape, dt)

        wshape = [(LAYERS, ND * ROWS[w], COLS[w]) for w in range(3)]
        scratch = [v(wshape[w], BF) for w in range(3)]
        scratch += [v((2, 2, 2, 2, ROWS[w], COLS[w]), F32) for w in range(3)]
        for lead in ((2, 2, 2), (2, 2), (2,), ()):
            scratch += [v((LAYERS,) + lead + (ROWS[w], COLS[w]), F32) for w in range(3)]
        scratch += [v((ND, LAYERS, 8, LN), F32), v((LAYERS, 8, DM), F32), v((LAYERS, 1, FF), F32),
                    v((LAYERS, 1, 3 * DM), F32), v((LAYERS, ND, 8, LN), F32), v((LAYERS, ND, 8, LN), F32),
                    v((8, DM), F32), v((1, FF), F32), v((1, 3 * DM), F32)]
        scratch += [v((SEQ, DM), BF), v((SEQ, DM), BF), v((SEQ, DM), BF), v((SEQ, DM), BF),
                    v((DM, SEQ), BF), v((DM, SEQ), BF), v((SEQ, 3 * DM), BF), v((SEQ, 3 * DM), BF),
                    v((SEQ, DM), BF), v((SEQ, DM), BF), v((SEQ, DM), F32), v((SEQ, DM), F32)]
        dma = pltpu.SemaphoreType.DMA
        scratch += [dma((LAYERS, 4)), dma((LAYERS, 3, 15)), dma((LAYERS, 3, 8)), dma((LAYERS, 3, 8)),
                    dma((LAYERS, 3, 4)), dma((LAYERS, 3, 4)), dma, dma, dma((LAYERS,)), dma((LAYERS,))]
        sds = jax.ShapeDtypeStruct
        y, xg, oa, ou, od, osm = pl.pallas_call(
            kernel,
            out_shape=[sds((SEQ, DM), BF), sds((SEQ, DM), BF), sds((LAYERS, SH, FF), BF),
                       sds((LAYERS, SH, FF), BF), sds((LAYERS, LN, DM), BF), sds((LAYERS, 8, LN), F32)],
            in_specs=[vm, vm, hbm, hbm, hbm, hbm, vm, vm, vm],
            out_specs=[vm] * 6,
            scratch_shapes=scratch,
            compiler_params=pltpu.CompilerParams(has_side_effects=True, vmem_limit_bytes=67043328),
            name='step',
        )(x[0], y_cot[0], wa, wup, wdn, small, *consts)
        gqkv = oa[:, :, :Q3].reshape(LAYERS, SH, 3, 8, HD).transpose(0, 1, 3, 2, 4).reshape(LAYERS, SH, 8, 192)
        sm = osm.astype(BF)
        return (y[None], xg[None], sm[:, 0, :SH], sm[:, 1, :SH], gqkv, sm[:, 7, :96], oa[:, :, Q3:], sm[:, 2, :SH],
                sm[:, 3, :SH], sm[:, 4, :SH], ou, sm[:, 6, :], od, sm[:, 5, :SH])

    return jax.shard_map(device_step, mesh=mesh,
                         in_specs=(act_spec, act_spec) + (param_spec,) * 12,
                         out_specs=(act_spec, act_spec) + (param_spec,) * 12,
                         check_vma=False)
```

time: 720 us -> 183 us (0.25); the launches traced: 712 us -> 183 us
  waiting for transfers between devices: 422 us -> 0 us
  Pallas kernels: 0 us -> 162 us
  blocking collectives: 119 us -> 0 us
  matrix products: 97.3 us -> 0 us
  other arithmetic: 27.4 us -> 1.33 us
  between operations: 15.6 us -> 0.75 us
  local copies, waits for them, and re-layouts: 29.4 us -> 18.7 us
    reduce_scatter x8 -> x0, waiting for transfers between devices: 393 us -> none  [scatter_grads(): lax.psum_scatter(grad_arr, shard_axes, scatter_dimension=0, tiled=True)]
    pallas_call x0 -> x1, Pallas kernels: none -> 162 us  [device_step(): pl.pallas_call(kernel, out_shape=[sds((SEQ, DM), BF), sds((SEQ, DM), BF),...]
    dot_general x32 -> x0, matrix products: 89.8 us -> none  [product(): jnp.einsum(einsum_form, first_op, second_op, preferred_element_type=jnp.f...]
    unnamed x2 -> x0, blocking collectives: 68.7 us -> none
    all_gather x4 -> x0, blocking collectives: 50.6 us -> none  [gather_layer(): lax.all_gather(tensor[layer_idx], shard_axes, axis=0, tiled=True)]
    all_gather x6 -> x0, waiting for transfers between devices: 27.2 us -> none  [gather_layer(): lax.all_gather(tensor[layer_idx], shard_axes, axis=0, tiled=True)]
    another operation x21 -> x0, other arithmetic: 13.3 us -> none  [the longest x19 12.7 us: device_step(): jnp.stack([layer_grads[i][j] for i in range(num_layers)])]
  transfers between devices with their start and end apart: 14 -> 0, of which waited for: 9 -> 0; matrix products, arithmetic and copies ran while one was open for 20% -> 0% of each run, Pallas kernels for 0% -> 0%
where the time goes in v1:
time: 183 us
  Pallas kernels  162 us (89%)
  local copies, waits for them, and re-layouts  18.7 us (10%)
    pallas_call x1, Pallas kernels, device_step(): pl.pallas_call(kernel, out_shape=[sds((SEQ, DM), BF), sds((SEQ, DM), BF),...  162 us
    unnamed x37, local copies, waits for them, and re-layouts  12.9 us

profile of v1, /device:TPU:0, one launch (start us, length us, event | category | flops | bytes accessed | tf_op | source)
XLA Modules:
  0.0 182.9 jit_solution(13676919881994252655)
XLA Ops:
  0.6 0.0 copy-start.6
  0.7 0.6 copy-done.6
  1.3 0.0 copy-start.7
  1.3 0.6 copy-done.7
  2.0 0.0 copy-start.8
  2.0 0.6 copy-done.8
  2.6 0.0 copy-start.9
  2.6 0.6 copy-done.9
  3.3 0.0 copy-start.10
  3.3 0.6 copy-done.10
  4.0 0.0 copy-start.11
  4.0 0.6 copy-done.11
  4.6 0.0 copy-start.12
  4.6 0.6 copy-done.12
  5.3 0.0 copy-start.13
  5.3 0.6 copy-done.13
  6.0 0.6 convert_element_type.15.small_in
  6.6 1.5 reshape.40
  8.0 0.1 copy.33
  8.1 0.0 copy-start.4
  8.1 0.3 reshape.41
  8.4 0.6 copy-done.4
  9.0 0.7 pad_maximum_fusion.wa_in
  9.7 162.2 %step.1 = (bf16[256,512]{1,0:T(8,128)(2,1)}, bf16[256,512]{1,0:T(8,128)(2,1)}, bf16[2,32,2048]{2,1,0:T(8,128)(2,1)}, bf16[2,32,2048]{2,1,0:T(8,128)(2,1)}, bf16[...) custom-call(bf16[256,512]{1,0:T(8,128)(2,1)} %bitcast.49, bf16[256,512]{1,0:T(8,128)(2,1)} %bitcast.50, ...), custom_call_target="tpu_custom_call" | custom-call | tf_op jit(solution)/shard_map/step/pallas_call | solution.py:504
  171.9 0.0 copy-start.5
  171.9 0.7 copy-done.5
  172.6 0.5 copy.62
  173.1 0.5 copy.61
  173.6 0.5 copy_bitcast_fusion.1
  174.1 0.5 copy_bitcast_fusion.4
  174.7 0.5 copy_bitcast_fusion.7
  175.2 1.5 slice.34
  176.7 0.9 slice.32
  177.6 0.2 reshape.42
  177.8 0.2 copy.60
  178.1 0.0 copy-start.3
  178.1 1.0 reshape.43
  179.1 0.0 copy-done.3
  179.1 0.0 copy-start.2
  179.1 0.7 copy.67
  179.8 0.3 copy-done.2
  180.1 0.0 copy-start.1
  180.1 0.7 copy.68
  180.8 0.3 copy-done.1
  181.2 0.0 copy-start
  181.2 0.7 copy.69
  181.9 0.3 copy-done
  182.2 0.7 copy.70
  (20 shorter events, 0.1 us)
Async XLA Ops:
  0.6 0.7 copy-start.6
  1.3 0.7 copy-start.7
  2.0 0.7 copy-start.8
  2.6 0.7 copy-start.9
  3.3 0.7 copy-start.10
  4.0 0.7 copy-start.11
  4.6 0.7 copy-start.12
  5.3 0.7 copy-start.13
  8.1 0.8 copy-start.4
  171.9 0.7 copy-start.5
  178.1 1.0 copy-start.3
  179.1 1.0 copy-start.2
  180.1 1.0 copy-start.1
  181.2 1.0 copy-start

commit v2 on v1

--- a/solution.py
+++ b/solution.py
@@ -15,6 +15,9 @@
 COLS = (FF, FF, DM)
 AO, UP, DN = 0, 1, 2
 ORDERS = ((1, 2, 4), (2, 4, 1), (4, 1, 2))
+CHIP_AXES = [4, 2, 1]
+HALVES = ((UP, 0), (UP, 1), (DN, 0), (DN, 1), (AO, 0), (AO, 1))
+UP0, UP1, DN0, DN1, AO0, AO1 = range(6)
 
 
 def bit(v, a):
@@ -40,14 +43,10 @@
     return lax.dot_general(a, b, (((0,), (0,)), ((), ())), preferred_element_type=F32)
 
 
-def axis_of(a, axes):
-    return axes.index(a)
-
-
-def kernel(x_ref, cot_ref, wa_in, wu_in, wd_in, small_in, rc_ref, r1_ref, r2_ref,
-           y_ref, xg_ref, oa_ref, ou_ref, od_ref, os_ref,
+def kernel(x_ref, cot_ref, wq_in, wo_in, wu_in, wd_in, p0, p1, p2, p3, p4, p5, p6, p7, rc_ref, r1_ref, r2_ref,
+           y_ref, xg_ref, oq_ref, oo_ref, ou_ref, od_ref, os_ref,
            wa, wu, wd, ga, gu, gd, ra0, ru0, rd0, ra1, ru1, rd1, ra2, ru2, rd2, ra3, ru3, rd3,
-           smalls, vec, upb, qkvb, gs, gr, gvec, gub, gqb,
+           smalls, v0, v1, v2, v3, v4, v5, v6, v7, vec, upb, qkvb, gs, gr, gvec, gub, gqb,
            h1, dh, na, nm, nat, nmt, qkv, dqkv, ctx, dctx, acc, dnm,
            loc_sem, ag_send, ag_ici, ag_d2d, rs_send, rs_recv, sm_send, sm_recv, gr_send, gr_recv):
     me = lax.axis_index('node') * 8 + lax.axis_index('local')
@@ -95,87 +94,102 @@
                                          recv_sem=ag_d2d.at[l, w, mask], device_id=dev(chip, other),
                                          device_id_type=MESH).wait_recv()
 
-    def ag0(l, w):
-        a, b, c = ORDERS[w]
-        to_link(l, w, 0, a)
-        to_link(l, w, 0, b)
-        to_link(l, w, 0, c)
-        to_partner(l, w, 0)
-
-    def ag1(l, w):
-        a, b, c = ORDERS[w]
-        got(l, w, a)
-        to_link(l, w, a, b)
-        to_link(l, w, a, c)
-        to_partner(l, w, a)
-
-    def ag2(l, w):
-        a, b, c = ORDERS[w]
-        for m in (b, a | b):
+    def ag0(l, ws):
+        for i in range(3):
+            for w in ws:
+                to_link(l, w, 0, ORDERS[w][i])
+        for w in ws:
+            to_partner(l, w, 0)
+
+    def ag1(l, ws):
+        for w in ws:
+            a, b, c = ORDERS[w]
+            got(l, w, a)
+            to_link(l, w, a, b)
+        for w in ws:
+            a, b, c = ORDERS[w]
+            to_link(l, w, a, c)
+            to_partner(l, w, a)
+
+    def ag2(l, ws, first):
+        for w in ws:
+            a, b, c = ORDERS[w]
+            m = b if first else a | b
             got(l, w, m)
             to_link(l, w, m, c)
             to_partner(l, w, m)
 
-    def ag3(l, w):
-        a, b, c = ORDERS[w]
-        for m in (c, a | c, b | c, 7):
-            got(l, w, m)
-            to_partner(l, w, m)
-
-    def rs_copy(l, w, stage, src, dst, to):
-        cp = pltpu.make_async_remote_copy(src_ref=src, dst_ref=dst, send_sem=rs_send.at[l, w, stage],
-                                          recv_sem=rs_recv.at[l, w, stage], device_id=to, device_id_type=MESH)
+    def ag3(l, ws):
+        for k in range(4):
+            for w in ws:
+                a, b, c = ORDERS[w]
+                m = (c, a | c, b | c, 7)[k]
+                got(l, w, m)
+                to_partner(l, w, m)
+
+    rs = {}
+
+    def rs_copy(l, g, stage, src, dst, to):
+        cp = pltpu.make_async_remote_copy(src_ref=src, dst_ref=dst, send_sem=rs_send.at[l, g, stage],
+                                          recv_sem=rs_recv.at[l, g, stage], device_id=to, device_id_type=MESH)
         cp.start()
-        return cp
-
-    rs = {}
-
-    def s0(l, w):
-        rs[l, w, 0] = rs_copy(l, w, 0, G[w].at[:, :, :, other], R0[w].at[l], dev(chip, other))
-
-    def pick(ax, n, v):
-        return tuple(v if i == ax else slice(None) for i in range(n))
-
-    def s1(l, w):
-        a, b, c = ORDERS[w]
-        rs[l, w, 0].wait_recv()
+        rs[l, g, stage] = cp
+
+    def half(g):
+        w, h = HALVES[g]
+        n = COLS[w] // 2
+        return w, ORDERS[g % 3], slice(n * h, n * h + n)
+
+    def pick(axes, a, v):
+        return tuple(v if m == a else slice(None) for m in axes)
+
+    def s0(l, g):
+        w, _, cs = half(g)
+        rs_copy(l, g, 0, G[w].at[:, :, :, other, :, cs], R0[w].at[l, :, :, :, :, cs], dev(chip, other))
+
+    def s1(l, g):
+        w, (a, b, c), cs = half(g)
+        rs[l, g, 0].wait_recv()
         for z in range(2):
             for y in range(2):
                 for x in range(2):
-                    R0[w][l, z, y, x] = R0[w][l, z, y, x] + G[w][z, y, x, core]
-        ax = axis_of(a, [4, 2, 1])
-        rs[l, w, 1] = rs_copy(l, w, 1, R0[w].at[(l,) + pick(ax, 3, 1 - bit(chip, a))], R1[w].at[l],
-                              dev(flip(chip, a), core))
-
-    def s2(l, w):
-        a, b, c = ORDERS[w]
-        rs[l, w, 1].wait_recv()
-        ax = axis_of(a, [4, 2, 1])
-        mine = bit(chip, a)
+                    R0[w][l, z, y, x, :, cs] = R0[w][l, z, y, x, :, cs] + G[w][z, y, x, core, :, cs]
+        src = R0[w].at[(l,) + pick(CHIP_AXES, a, 1 - bit(chip, a)) + (slice(None), cs)]
+        rs_copy(l, g, 1, src, R1[w].at[l, :, :, :, cs], dev(flip(chip, a), core))
+
+    def s2(l, g):
+        w, (a, b, c), cs = half(g)
+        rs[l, g, 1].wait_recv()
+        left = [m for m in CHIP_AXES if m != a]
         for i in range(2):
             for j in range(2):
                 idx = [i, j]
-                idx.insert(ax, mine)
-                R1[w][l, i, j] = R1[w][l, i, j] + R0[w][(l,) + tuple(idx)]
-        ax = axis_of(b, [m for m in (4, 2, 1) if m != a])
-        rs[l, w, 2] = rs_copy(l, w, 2, R1[w].at[(l,) + pick(ax, 2, 1 - bit(chip, b))], R2[w].at[l],
-                              dev(flip(chip, b), core))
-
-    def s3(l, w):
-        a, b, c = ORDERS[w]
-        rs[l, w, 2].wait_recv()
-        ax = axis_of(b, [m for m in (4, 2, 1) if m != a])
-        mine = bit(chip, b)
+                idx.insert(CHIP_AXES.index(a), bit(chip, a))
+                R1[w][l, i, j, :, cs] = R1[w][l, i, j, :, cs] + R0[w][(l,) + tuple(idx) + (slice(None), cs)]
+        src = R1[w].at[(l,) + pick(left, b, 1 - bit(chip, b)) + (slice(None), cs)]
+        rs_copy(l, g, 2, src, R2[w].at[l, :, :, cs], dev(flip(chip, b), core))
+
+    def s3(l, g):
+        w, (a, b, c), cs = half(g)
+        rs[l, g, 2].wait_recv()
+        left = [m for m in CHIP_AXES if m != a]
         for i in range(2):
             idx = [i]
-            idx.insert(ax, mine)
-            R2[w][l, i] = R2[w][l, i] + R1[w][(l,) + tuple(idx)]
-        rs[l, w, 3] = rs_copy(l, w, 3, R2[w].at[l, 1 - bit(chip, c)], R3[w].at[l], dev(flip(chip, c), core))
-
-    def s4(l, w):
-        c = ORDERS[w][2]
-        rs[l, w, 3].wait_recv()
-        (oa_ref, ou_ref, od_ref)[w][l] = (R3[w][l] + R2[w][l, bit(chip, c)]).astype(BF)
+            idx.insert(left.index(b), bit(chip, b))
+            R2[w][l, i, :, cs] = R2[w][l, i, :, cs] + R1[w][(l,) + tuple(idx) + (slice(None), cs)]
+        rs_copy(l, g, 3, R2[w].at[l, 1 - bit(chip, c), :, cs], R3[w].at[l, :, cs], dev(flip(chip, c), core))
+
+    def s4(l, g):
+        w, (a, b, c), cs = half(g)
+        rs[l, g, 3].wait_recv()
+        total = (R3[w][l, :, cs] + R2[w][l, bit(chip, c), :, cs]).astype(BF)
+        if g == AO1:
+            oq_ref[l, :, 2 * DM:] = total[:, :DM]
+            oo_ref[l] = total[:, DM:]
+        elif g == AO0:
+            oq_ref[l, :, cs] = total
+        else:
+            (None, ou_ref, od_ref)[w][l, :, cs] = total
 
     def normed(h_bf, l):
         h32 = h_bf.astype(F32)
@@ -249,7 +263,7 @@
 
         lax.fori_loop(0, 4, body, 0)
 
-    def mlp(l, dout, fwd):
+    def mlp(l, dout, fwd, middle):
         if fwd:
             acc[...] = jnp.zeros_like(acc)
         if dout is not None:
@@ -277,13 +291,18 @@
                 dnm[...] += mm_nt(dpb, wu_t)
             return carry
 
-        lax.fori_loop(0, 4, body, 0)
+        lax.fori_loop(0, 2, body, 0)
+        middle()
+        lax.fori_loop(2, 4, body, 0)
 
     def attn_grads(l, dout):
-        ga[:, :, :, :, :, Q3:FF] = mm_tn(ctx[...], dout[...]).reshape(2, 2, 2, 2, SH, DM)
-        for t in range(3):
+        ga[:, :, :, :, :, Q3:] = mm_tn(ctx[...], dout[...]).reshape(2, 2, 2, 2, SH, DM)
+        for t in (2, 0, 1):
             cols = slice(DM * t, DM * t + DM)
             ga[:, :, :, :, :, cols] = mm(nat[...], dqkv[:, cols]).reshape(2, 2, 2, 2, SH, DM)
+            if t == 2:
+                s0(l, AO1)
+        s0(l, AO0)
 
     def layer_end(h_ref, l, dout):
         dna = mm_nt(dqkv[...], wa[l, :, 0:Q3]).astype(BF).astype(F32)
@@ -338,17 +357,22 @@
             total = total + gr[l, d]
         os_ref[l] = total
 
-    local = []
-    for w, src in enumerate((wa_in, wu_in, wd_in)):
-        for l in range(LAYERS):
-            cp = pltpu.make_async_copy(src.at[l], block(l, w, chip, core), loc_sem.at[l, w])
+    def place(l):
+        cps = []
+        qo = pl.multiple_of(me * SH, SH)
+        pairs = [(wq_in, W[AO].at[l, pl.ds(qo, SH), pl.ds(0, Q3)]), (wo_in, W[AO].at[l, pl.ds(qo, SH), pl.ds(Q3, DM)]),
+                 (wu_in, block(l, UP, chip, core)), (wd_in, block(l, DN, chip, core))]
+        for i, (src, dst) in enumerate(pairs):
+            cps.append(pltpu.make_async_copy(src.at[l], dst, loc_sem.at[l, i]))
+        for cp in cps:
             cp.start()
-            local.append(cp)
-    cp = pltpu.make_async_copy(small_in, smalls.at[me], loc_sem.at[0, 3])
-    cp.start()
-    local.append(cp)
-    for cp in local:
-        cp.wait()
+        return cps
+
+    first, second = place(0), place(1)
+    params, tmp = (p0, p1, p2, p3, p4, p5, p6, p7), (v0, v1, v2, v3, v4, v5, v6, v7)
+    little = [pltpu.make_async_copy(params[i], tmp[i], loc_sem.at[2 + i // 4, i % 4]) for i in range(8)]
+    for cp in little:
+        cp.start()
 
     def send_small(i, carry):
         t, to = peer(i)
@@ -356,17 +380,24 @@
                                      recv_sem=sm_recv, device_id=to, device_id_type=MESH).start()
         return carry
 
-    groups = (AO, UP, DN)
-    for w in groups:
-        ag0(0, w)
+    groups = (UP, DN, AO)
+    for cp in first:
+        cp.wait()
+    ag0(0, groups)
+    for i in range(8):
+        little[i].wait()
+        for l in range(LAYERS):
+            smalls[me, l, i:i + 1, 0:tmp[i].shape[1]] = tmp[i][l:l + 1, :].astype(F32)
     lax.fori_loop(1, ND, send_small, 0)
-    for w in groups:
-        ag1(0, w)
+    for cp in second:
+        cp.wait()
+    ag1(0, groups)
     whole = pltpu.make_async_remote_copy(src_ref=smalls.at[pl.ds(0, ND - 1)], dst_ref=smalls.at[pl.ds(0, ND - 1)],
                                          send_sem=sm_send, recv_sem=sm_recv, device_id=dev(chip, other),
                                          device_id_type=MESH)
     whole.wait_send()
     whole.wait_recv()
+    ag2(0, groups, True)
     for l in range(LAYERS):
         for d in range(ND):
             vec[l, 0:6, SH * d:SH * d + SH] = smalls[d, l, 0:6, 0:SH]
@@ -374,83 +405,94 @@
             for lo, col, n in bias_parts(d):
                 qkvb[l, 0:1, col:col + n] = smalls[d, l, 7:8, lo:lo + n]
     norms(x_ref, 0, False)
-    for w in groups:
-        ag2(0, w)
-    for w in groups:
-        ag0(1, w)
-    for w in groups:
-        ag3(0, w)
-    for w in groups:
-        ag1(1, w)
+    ag2(0, groups, False)
+    ag0(1, groups)
+    ag3(0, (AO, UP, DN))
     got_partner(0, AO)
     make_qkv(0)
+    ag1(1, groups)
     heads(0, False)
-    for w in groups:
-        ag2(1, w)
+    ag2(1, groups, True)
     got_partner(0, UP)
     got_partner(0, DN)
-    mlp(0, None, True)
-    acc[...] += mm(ctx[...], wa[0, :, Q3:FF])
+    mlp(0, None, True, lambda: None)
+    ag2(1, groups, False)
+    acc[...] += mm(ctx[...], wa[0, :, Q3:])
     h1[...] = (x_ref[...].astype(F32) + acc[...] + vec[0, 2:3, :] + vec[0, 5:6, :]).astype(BF)
 
     norms(h1, 1, True)
-    ag3(1, UP)
-    ag3(1, DN)
+    ag3(1, groups)
     got_partner(1, UP)
     got_partner(1, DN)
-    mlp(1, cot_ref, True)
-    s0(1, DN)
-    s0(1, UP)
-    ag3(1, AO)
+    mlp(1, cot_ref, True, lambda: s0(1, UP0))
+    for g in (UP1, DN0, DN1):
+        s0(1, g)
+    s1(1, UP0)
     got_partner(1, AO)
     make_qkv(1)
-    dctx[...] = mm_nt(cot_ref[...], wa[1, :, Q3:FF]).astype(BF)
-    s1(1, DN)
-    s1(1, UP)
+    dctx[...] = mm_nt(cot_ref[...], wa[1, :, Q3:]).astype(BF)
+    for g in (UP1, DN0, DN1):
+        s1(1, g)
     heads(1, True)
     attn_grads(1, cot_ref)
-    s0(1, AO)
-    acc[...] += mm(ctx[...], wa[1, :, Q3:FF])
+    acc[...] += mm(ctx[...], wa[1, :, Q3:])
     y_ref[...] = (h1[...].astype(F32) + acc[...] + vec[1, 2:3, :] + vec[1, 5:6, :]).astype(BF)
+    s1(1, AO1)
+    s1(1, AO0)
     dh[...] = layer_end(h1, 1, cot_ref)
     small_grads(1)
     small_send(1)
-    s1(1, AO)
 
     norms(x_ref, 0, True)
-    rs[1, DN, 0].wait_send()
-    rs[1, UP, 0].wait_send()
-    mlp(0, dh, False)
-    s0(0, DN)
-    s0(0, UP)
+    for g in (UP0, UP1, DN0, DN1):
+        rs[1, g, 0].wait_send()
+    mlp(0, dh, False, lambda: s0(0, UP0))
+    for g in (UP1, DN0, DN1):
+        s0(0, g)
+    s1(0, UP0)
+    for g in (UP0, UP1, DN0):
+        s2(1, g)
     make_qkv(0)
-    dctx[...] = mm_nt(dh[...], wa[0, :, Q3:FF]).astype(BF)
-    s1(0, DN)
-    s1(0, UP)
+    dctx[...] = mm_nt(dh[...], wa[0, :, Q3:]).astype(BF)
+    for g in (UP1, DN0, DN1):
+        s1(0, g)
     heads(0, True)
-    rs[1, AO, 0].wait_send()
+    s2(1, DN1)
+    for g in (AO0, AO1):
+        rs[1, g, 0].wait_send()
     attn_grads(0, dh)
-    s0(0, AO)
     xg_ref[...] = layer_end(x_ref, 0, dh)
+    s1(0, AO1)
+    s1(0, AO0)
     small_grads(0)
     small_send(0)
-    s1(0, AO)
-    order = ((1, DN), (1, UP), (1, AO), (0, DN), (0, UP), (0, AO))
-    for l, w in order:
-        s2(l, w)
-    for l, w in order:
-        s3(l, w)
-    for l, w in order:
-        s4(l, w)
+    mlp_halves, attn_halves = (UP0, UP1, DN0, DN1), (AO1, AO0)
+    for stage, l, gs_ in ((s2, 1, attn_halves), (s3, 1, mlp_halves), (s2, 0, mlp_halves), (s3, 1, attn_halves),
+                          (s2, 0, attn_halves), (s3, 0, mlp_halves), (s4, 1, mlp_halves), (s4, 1, attn_halves),
+                          (s3, 0, attn_halves), (s4, 0, mlp_halves), (s4, 0, attn_halves)):
+        for g in gs_:
+            stage(l, g)
     small_finish(1)
     small_finish(0)
-    for w in groups:
-        rs[0, w, 0].wait_send()
+    for g in range(6):
+        rs[0, g, 0].wait_send()
         for l in range(LAYERS):
             for stage in range(1, 4):
-                rs[l, w, stage].wait_send()
+                rs[l, g, stage].wait_send()
     for cp in pend:
         cp.wait_send()
+
+
+def finish(y, xg, oo, ou, od, osm, *outs):
+    yo, xo, g1, b1, bq, go, bo, g2, b2, gup, bu, gdn, bd = outs
+    yo[0] = y[...]
+    xo[0] = xg[...]
+    go[...] = oo[...]
+    gup[...] = ou[...]
+    gdn[...] = od[...]
+    for row, ref in enumerate((g1, b1, bo, g2, b2, bd, bu, bq)):
+        for l in range(LAYERS):
+            ref[l:l + 1, :] = osm[l, row:row + 1, 0:ref.shape[1]].astype(BF)
 
 
 def rope_constants():
@@ -478,10 +520,8 @@
     hbm = pl.BlockSpec(memory_space=pl.ANY)
 
     def device_step(x, y_cot, g1, b1, wqkv, bqkv, wout, bout, g2, b2, wup, bup, wdn, bdn):
-        qkv_cols = wqkv.reshape(LAYERS, SH, 8, 3, HD).transpose(0, 1, 3, 2, 4).reshape(LAYERS, SH, Q3)
-        wa = jnp.concatenate([qkv_cols, wout], axis=-1)
-        small = jnp.stack([jnp.pad(v, ((0, 0), (0, LN - v.shape[1])))
-                           for v in (g1, b1, bout, g2, b2, bdn, bup, bqkv)], axis=1).astype(F32)
+        wq = wqkv.reshape(LAYERS, SH, 8, 3, HD).transpose(0, 1, 3, 2, 4).reshape(LAYERS, SH, Q3)
+        little = (g1, b1, bout, g2, b2, bdn, bup, bqkv)
 
         def v(shape, dt):
             return pltpu.VMEM(shape, dt)
@@ -491,30 +531,33 @@
         scratch += [v((2, 2, 2, 2, ROWS[w], COLS[w]), F32) for w in range(3)]
         for lead in ((2, 2, 2), (2, 2), (2,), ()):
             scratch += [v((LAYERS,) + lead + (ROWS[w], COLS[w]), F32) for w in range(3)]
-        scratch += [v((ND, LAYERS, 8, LN), F32), v((LAYERS, 8, DM), F32), v((LAYERS, 1, FF), F32),
+        scratch += [v((ND, LAYERS, 8, LN), F32)] + [v(p.shape, BF) for p in little]
+        scratch += [v((LAYERS, 8, DM), F32), v((LAYERS, 1, FF), F32),
                     v((LAYERS, 1, 3 * DM), F32), v((LAYERS, ND, 8, LN), F32), v((LAYERS, ND, 8, LN), F32),
                     v((8, DM), F32), v((1, FF), F32), v((1, 3 * DM), F32)]
         scratch += [v((SEQ, DM), BF), v((SEQ, DM), BF), v((SEQ, DM), BF), v((SEQ, DM), BF),
                     v((DM, SEQ), BF), v((DM, SEQ), BF), v((SEQ, 3 * DM), BF), v((SEQ, 3 * DM), BF),
                     v((SEQ, DM), BF), v((SEQ, DM), BF), v((SEQ, DM), F32), v((SEQ, DM), F32)]
         dma = pltpu.SemaphoreType.DMA
-        scratch += [dma((LAYERS, 4)), dma((LAYERS, 3, 15)), dma((LAYERS, 3, 8)), dma((LAYERS, 3, 8)),
-                    dma((LAYERS, 3, 4)), dma((LAYERS, 3, 4)), dma, dma, dma((LAYERS,)), dma((LAYERS,))]
+        scratch += [dma((4, 4)), dma((LAYERS, 3, 15)), dma((LAYERS, 3, 8)), dma((LAYERS, 3, 8)),
+                    dma((LAYERS, 6, 4)), dma((LAYERS, 6, 4)), dma, dma, dma((LAYERS,)), dma((LAYERS,))]
         sds = jax.ShapeDtypeStruct
-        y, xg, oa, ou, od, osm = pl.pallas_call(
+        mids = pl.pallas_call(
             kernel,
-            out_shape=[sds((SEQ, DM), BF), sds((SEQ, DM), BF), sds((LAYERS, SH, FF), BF),
+            out_shape=[sds((SEQ, DM), BF), sds((SEQ, DM), BF), sds((LAYERS, SH, Q3), BF), sds((LAYERS, SH, DM), BF),
                        sds((LAYERS, SH, FF), BF), sds((LAYERS, LN, DM), BF), sds((LAYERS, 8, LN), F32)],
-            in_specs=[vm, vm, hbm, hbm, hbm, hbm, vm, vm, vm],
-            out_specs=[vm] * 6,
+            in_specs=[vm, vm] + [hbm] * 12 + [vm] * 3,
+            out_specs=[vm] * 7,
             scratch_shapes=scratch,
             compiler_params=pltpu.CompilerParams(has_side_effects=True, vmem_limit_bytes=67043328),
             name='step',
-        )(x[0], y_cot[0], wa, wup, wdn, small, *consts)
-        gqkv = oa[:, :, :Q3].reshape(LAYERS, SH, 3, 8, HD).transpose(0, 1, 3, 2, 4).reshape(LAYERS, SH, 8, 192)
-        sm = osm.astype(BF)
-        return (y[None], xg[None], sm[:, 0, :SH], sm[:, 1, :SH], gqkv, sm[:, 7, :96], oa[:, :, Q3:], sm[:, 2, :SH],
-                sm[:, 3, :SH], sm[:, 4, :SH], ou, sm[:, 6, :], od, sm[:, 5, :SH])
+        )(x[0], y_cot[0], wq, wout, wup, wdn, *little, *consts)
+        y, xg, oq, oo, ou, od, osm = mids
+        gqkv = oq.reshape(LAYERS, SH, 3, 8, HD).transpose(0, 1, 3, 2, 4).reshape(LAYERS, SH, 8, 3 * HD)
+        like = (x, y_cot, g1, b1, bqkv, wout, bout, g2, b2, wup, bup, wdn, bdn)
+        outs = pl.pallas_call(finish, out_shape=[sds(p.shape, BF) for p in like], in_specs=[vm] * 6,
+                              out_specs=[vm] * 13, name='finish')(y, xg, oo, ou, od, osm)
+        return tuple(outs[:4]) + (gqkv,) + tuple(outs[4:])
 
     return jax.shard_map(device_step, mesh=mesh,
                          in_specs=(act_spec, act_spec) + (param_spec,) * 12,

time: 183 us -> 155 us (0.85)
  local copies, waits for them, and re-layouts: 18.7 us -> 3.95 us
  Pallas kernels: 162 us -> 150 us
    pallas_call x1, Pallas kernels: 162 us -> 147 us  [device_step(): pl.pallas_call(kernel, out_shape=[sds((SEQ, DM), BF), sds((SEQ, DM), BF),...]
    unnamed x37 -> x2, local copies, waits for them, and re-layouts: 12.9 us -> 0.01 us
    slice x5 -> x0, local copies, waits for them, and re-layouts: 2.43 us -> none  [the longest x1 1.47 us: device_step(): oa[:, :, Q3:]]
    pallas_call x0 -> x1, Pallas kernels: none -> 2.26 us  [device_step(): pl.pallas_call(finish, out_shape=[sds(p.shape, BF) for p in like], in_spe...]
where the time goes in v2:
time: 155 us; the launch traced here: 154 us
  Pallas kernels  150 us (97%)
  local copies, waits for them, and re-layouts  3.95 us (3%)
    pallas_call x1, Pallas kernels, device_step(): pl.pallas_call(kernel, out_shape=[sds((SEQ, DM), BF), sds((SEQ, DM), BF),...  147 us

profile of v2, /device:TPU:0, one launch (start us, length us, event | category | flops | bytes accessed | tf_op | source)
XLA Modules:
  0.0 154.4 jit_solution(10471162083113600396)
XLA Ops:
  0.6 1.5 reshape.40
  2.1 0.1 copy.33
  2.2 0.9 reshape.41.wq_in
  3.1 147.5 %step.1 = (bf16[256,512]{1,0:T(8,128)(2,1)}, bf16[256,512]{1,0:T(8,128)(2,1)}, bf16[2,32,1536]{2,1,0:T(8,128)(2,1)}, bf16[2,32,512]{2,1,0:T(8,128)(2,1)}, bf16[2...) custom-call(bf16[256,512]{1,0:T(8,128)(2,1)} %bitcast.12, bf16[256,512]{1,0:T(8,128)(2,1)} %bitcast.13, ...), custom_call_target="tpu_custom_call" | custom-call | tf_op jit(solution)/shard_map/step/pallas_call | solution.py:545
  150.6 0.0 copy-start
  150.6 2.3 %finish.1 = (bf16[1,256,512]{2,1,0:T(8,128)(2,1)}, bf16[1,256,512]{2,1,0:T(8,128)(2,1)}, bf16[2,32]{1,0:T(2,128)(2,1)}, bf16[2,32]{1,0:T(2,128)(2,1)}, bf16[2,96...) custom-call(bf16[256,512]{1,0:T(8,128)(2,1)} %get-tuple-element.34.y, ...), custom_call_target="tpu_custom_call" | custom-call | tf_op jit(solution)/shard_map/finish/pallas_call | solution.py:558
  152.9 0.0 copy-done
  152.9 0.2 reshape.42
  153.2 0.2 copy.36
  153.4 1.0 reshape.43
Async XLA Ops:
  150.6 2.3 %copy-start = (bf16[2,32,1536]{2,1,0:T(8,128)(2,1)S(1)}, bf16[2,32,1536]{2,1,0:T(8,128)(2,1)}, u32[]{:S(2)}) copy-start(bf16[2,32,1536]{2,1,0:T(8,128)(2,1)} %get-tuple-element.44) | copy-start | bytes 589828

commit v3 on v1

v3 whole, which is shorter than its diff:
```python
import numpy as np
import jax
import jax.numpy as jnp
from jax import lax
from jax.experimental import pallas as pl
from jax.experimental.pallas import tpu as pltpu
from jax.sharding import PartitionSpec as P

BF, F32 = jnp.bfloat16, jnp.float32
MESH = pl.DeviceIdType.MESH
EPSILON = 1e-5
LAYERS, SEQ, DM, FF, ND = 2, 256, 512, 2048, 16
SH, HD, LN, Q3 = 32, 64, 128, 1536
ROWS = (SH, SH, LN)
COLS = (FF, FF, DM)
AO, UP, DN = 0, 1, 2
ORDERS = ((1, 2, 4), (2, 4, 1), (4, 1, 2))
CHIP_AXES = [4, 2, 1]
CUTS = ((0, 640, 1280, FF), (0, 640, 1280, FF), (0, 48, 96, LN))
ALL, EV = slice(None), ...


def piece(w, k):
    lo, hi = CUTS[w][k], CUTS[w][k + 1]
    return (slice(lo, hi), ALL) if w == DN else (ALL, slice(lo, hi))


def bit(v, a):
    return lax.rem(lax.div(v, a), 2)


def flip(v, mask):
    for a in (1, 2, 4):
        if mask & a:
            v = v + a - 2 * a * bit(v, a)
    return v


def col_sum(v):
    return jnp.sum(v, axis=0, keepdims=True)


def row_of(f, v):
    return f(v, axis=-1, keepdims=True)


def mm(a, b):
    return jnp.dot(a, b, preferred_element_type=F32)


def mm_nt(a, b):
    return lax.dot_general(a, b, (((1,), (1,)), ((), ())), preferred_element_type=F32)


def mm_tn(a, b):
    return lax.dot_general(a, b, (((0,), (0,)), ((), ())), preferred_element_type=F32)


def kernel(x_in, cot_in, wq_in, wo_in, wu_in, wd_in, p0, p1, p2, p3, p4, p5, p6, p7, rope_in,
           y_ref, xg_ref, oq_ref, oo_ref, ou_ref, od_ref, os_ref,
           wa, wu, wd, ga, gu, gd, ra0, ru0, rd0, ra1, ru1, rd1, ra2, ru2, rd2, ra3, ru3, rd3,
           smalls, v0, v1, v2, v3, v4, v5, v6, v7, vec, upb, qkvb, gs, gr, gvec, gub, gqb,
           x_ref, cot_ref, rope_ref, native, spread, act_s, slope_s,
           h1, dh, na, nm, nat, nmt, qkv, dqkv, ctx, dctx, acc, dnm,
           loc_sem, ag_send, ag_ici, ag_d2d, rs_send, rs_recv, sm_send, sm_recv, gr_send, gr_recv):
    me = lax.axis_index('node') * 8 + lax.axis_index('local')
    chip = lax.div(me, 2)
    core = lax.rem(me, 2)
    other = 1 - core
    W, G = (wa, wu, wd), (ga, gu, gd)
    R0, R1, R2, R3 = (ra0, ru0, rd0), (ra1, ru1, rd1), (ra2, ru2, rd2), (ra3, ru3, rd3)

    def dev(c, k):
        i = c * 2 + k
        return (lax.div(i, 8), lax.rem(i, 8))

    def block(l, w, c, k):
        return W[w].at[l, pl.ds(pl.multiple_of((c * 2 + k) * ROWS[w], ROWS[w]), ROWS[w])]

    def part(l, w, k, mask):
        base = (flip(chip, mask) * 2 + core) * ROWS[w]
        rs_, cs = piece(w, k)
        if w == DN:
            n = rs_.stop - rs_.start
            return W[w].at[l, pl.ds(pl.multiple_of(base + rs_.start, 16), n)]
        return W[w].at[l, pl.ds(pl.multiple_of(base, SH), SH), cs]

    def push(l, w, src, to, recv_sem):
        pltpu.make_async_remote_copy(src_ref=src, dst_ref=src, send_sem=ag_send.at[l, w], recv_sem=recv_sem,
                                     device_id=to, device_id_type=MESH).start()

    def to_link(l, w, k, mask, a):
        push(l, w, part(l, w, k, mask), dev(flip(chip, a), core), ag_ici.at[l, w, k, mask ^ a])

    def to_partner(l, w, k, mask):
        push(l, w, part(l, w, k, mask), dev(chip, other), ag_d2d.at[l, w])

    def await_in(l, w, src, recv_sem):
        pltpu.make_async_remote_copy(src_ref=src, dst_ref=src, send_sem=ag_send.at[l, w], recv_sem=recv_sem,
                                     device_id=dev(chip, other), device_id_type=MESH).wait_recv()

    def got(l, w, k, mask):
        await_in(l, w, part(l, w, k, mask), ag_ici.at[l, w, k, mask])

    def got_partner(l, w):
        await_in(l, w, W[w].at[l, pl.ds(0, 8 * ROWS[w])], ag_d2d.at[l, w])

    def sent(l, w):
        src = W[w].at[l, pl.ds(0, 15 * ROWS[w])]
        pltpu.make_async_remote_copy(src_ref=src, dst_ref=src, send_sem=ag_send.at[l, w], recv_sem=ag_d2d.at[l, w],
                                     device_id=dev(chip, other), device_id_type=MESH).wait_send()

    def own(l, w):
        for i in range(3):
            for k in range(3):
                to_link(l, w, k, 0, ORDERS[k][i])
        push(l, w, block(l, w, chip, core), dev(chip, other), ag_d2d.at[l, w])

    def f1(l, w):
        for k, (a, b, c) in enumerate(ORDERS):
            got(l, w, k, a)
            to_link(l, w, k, a, b)
        for k, (a, b, c) in enumerate(ORDERS):
            to_link(l, w, k, a, c)
            to_partner(l, w, k, a)

    def f2(l, w):
        for k, (a, b, c) in enumerate(ORDERS):
            got(l, w, k, b)
            to_link(l, w, k, b, c)
            to_partner(l, w, k, b)

    def f3(l, w):
        for k, (a, b, c) in enumerate(ORDERS):
            got(l, w, k, a | b)
            to_link(l, w, k, a | b, c)
            to_partner(l, w, k, a | b)

    def f4(l, w):
        for i in range(4):
            for k, (a, b, c) in enumerate(ORDERS):
                m = (c, a | c, b | c, 7)[i]
                got(l, w, k, m)
                to_partner(l, w, k, m)

    rs = {}

    def rs_copy(l, w, k, stage, src, dst, to):
        cp = pltpu.make_async_remote_copy(src_ref=src, dst_ref=dst, send_sem=rs_send.at[l, w, k, stage],
                                          recv_sem=rs_recv.at[l, w, k, stage], device_id=to, device_id_type=MESH)
        cp.start()
        rs[l, w, k, stage] = cp

    def pick(axes, a, v):
        return tuple(v if m == a else ALL for m in axes)

    def drained(l, w, stage):
        for k in range(3):
            rs[l, w, k, stage].wait_send()

    def s0(l, w):
        for k in range(3):
            cut = piece(w, k)
            rs_copy(l, w, k, 0, G[w].at[(ALL, ALL, ALL, other) + cut], R0[w].at[(l, ALL, ALL, ALL) + cut],
                    dev(chip, other))

    def s1(l, w):
        for k, (a, b, c) in enumerate(ORDERS):
            cut = piece(w, k)
            rs[l, w, k, 0].wait_recv()
            for z in range(2):
                for y in range(2):
                    for x in range(2):
                        at = (l, z, y, x) + cut
                        R0[w][at] = R0[w][at] + G[w][(z, y, x, core) + cut]
            src = R0[w].at[(l,) + pick(CHIP_AXES, a, 1 - bit(chip, a)) + cut]
            rs_copy(l, w, k, 1, src, R1[w].at[(l, ALL, ALL) + cut], dev(flip(chip, a), core))

    def s2(l, w):
        for k, (a, b, c) in enumerate(ORDERS):
            cut = piece(w, k)
            rs[l, w, k, 1].wait_recv()
            left = [m for m in CHIP_AXES if m != a]
            for i in range(2):
                for j in range(2):
                    idx = [i, j]
                    idx.insert(CHIP_AXES.index(a), bit(chip, a))
                    at = (l, i, j) + cut
                    R1[w][at] = R1[w][at] + R0[w][(l,) + tuple(idx) + cut]
            src = R1[w].at[(l,) + pick(left, b, 1 - bit(chip, b)) + cut]
            rs_copy(l, w, k, 2, src, R2[w].at[(l, ALL) + cut], dev(flip(chip, b), core))

    def s3(l, w):
        for k, (a, b, c) in enumerate(ORDERS):
            cut = piece(w, k)
            rs[l, w, k, 2].wait_recv()
            left = [m for m in CHIP_AXES if m != a]
            for i in range(2):
                idx = [i]
                idx.insert(left.index(b), bit(chip, b))
                at = (l, i) + cut
                R2[w][at] = R2[w][at] + R1[w][(l,) + tuple(idx) + cut]
            rs_copy(l, w, k, 3, R2[w].at[(l, 1 - bit(chip, c)) + cut], R3[w].at[(l,) + cut], dev(flip(chip, c), core))

    def s4(l, w):
        for k, (a, b, c) in enumerate(ORDERS):
            cut = piece(w, k)
            rs[l, w, k, 3].wait_recv()
            total = (R3[w][(l,) + cut] + R2[w][(l, bit(chip, c)) + cut]).astype(BF)
            if w != AO:
                (None, ou_ref, od_ref)[w][(l,) + cut] = total
            elif k < 2:
                oq_ref[(l,) + cut] = total
            else:
                n = Q3 - cut[1].start
                oq_ref[l, :, cut[1].start:] = total[:, :n]
                oo_ref[l] = total[:, n:]

    def normed(h_bf, l):
        h32 = h_bf.astype(F32)
        cen = h32 - row_of(jnp.mean, h32)
        rstd = lax.rsqrt(row_of(jnp.mean, cen * cen) + EPSILON)
        return cen * rstd, rstd

    def norms(h_ref, l, bwd):
        xhat, _ = normed(h_ref[EV], l)
        n1 = (xhat * vec[l, 0:1, :] + vec[l, 1:2, :]).astype(BF)
        n2 = (xhat * vec[l, 3:4, :] + vec[l, 4:5, :]).astype(BF)
        na[EV] = n1
        nm[EV] = n2
        if bwd:
            nat[EV] = n1.T
            nmt[EV] = n2.T

    def rope(xs, back):
        c, p, q = rope_ref[0], rope_ref[1], rope_ref[2]
        if back:
            return xs * c + pltpu.roll(xs * p, 8, 1) + pltpu.roll(xs * q, 120, 1)
        return xs * c + pltpu.roll(xs, 120, 1) * p + pltpu.roll(xs, 8, 1) * q

    def make_qkv(l):
        for t in range(3):
            cols = slice(DM * t, DM * t + DM)
            raw = mm(na[EV], wa[l, :, cols]) + qkvb[l, :, cols]
            for s in range(4):
                part = raw[:, LN * s:LN * s + LN]
                if t < 2:
                    part = rope(part, False)
                qkv[:, DM * t + LN * s:DM * t + LN * s + LN] = part.astype(BF)

    def heads(bwd, lo, hi):
        lane = lax.broadcasted_iota(jnp.int32, (1, LN), 1)
        masks = [(lane < HD).astype(F32).astype(BF), (lane >= HD).astype(F32).astype(BF)]
        causal = (lax.broadcasted_iota(jnp.int32, (SEQ, SEQ), 0) >= lax.broadcasted_iota(jnp.int32, (SEQ, SEQ), 1))

        def body(j, carry):
            col = pl.multiple_of(j * LN, LN)
            q, k, v = (qkv[:, pl.ds(col + DM * t, LN)] for t in range(3))
            ctx_sum = jnp.zeros((SEQ, LN), F32)
            if bwd:
                dc = dctx[:, pl.ds(col, LN)]
                dq = jnp.zeros((SEQ, LN), F32)
                dk = jnp.zeros((SEQ, LN), F32)
                dv = jnp.zeros((SEQ, LN), F32)
            for mask in masks:
                qm = q * mask
                sc = jnp.where(causal, mm_nt(qm, k) * 0.125, -1e30)
                e = jnp.exp(sc - row_of(jnp.max, sc))
                p = e / row_of(jnp.sum, e)
                pb = p.astype(BF)
                ctx_sum = ctx_sum + mm(pb, v * mask)
                if bwd:
                    dcm = dc * mask
                    dp = mm_nt(dcm, v).astype(BF).astype(F32)
                    dv = dv + mm_tn(pb, dcm)
                    ds = (p * (dp - row_of(jnp.sum, dp * p)) * 0.125).astype(BF)
                    dq = dq + mm(ds, k * mask)
                    dk = dk + mm_tn(ds, qm)
            ctx[:, pl.ds(col, LN)] = ctx_sum.astype(BF)
            if bwd:
                for t, d in enumerate((dq, dk, dv)):
                    d = d.astype(BF).astype(F32)
                    if t < 2:
                        d = rope(d, True)
                    gqb[0:1, pl.ds(col + DM * t, LN)] = col_sum(d)
                    dqkv[:, pl.ds(col + DM * t, LN)] = d.astype(BF)
            return carry

        lax.fori_loop(lo, hi, body, 0)

    def up_part(l, t):
        col = pl.multiple_of(t * DM, DM)
        pre = mm(nm[EV], wu[l, :, pl.ds(col, DM)]) + upb[l, :, pl.ds(col, DM)]
        cdf = 0.5 * (1.0 + lax.erf(pre * 0.7071067811865476))
        return col, pre, cdf, (pre * cdf).astype(BF)

    def mlp_fwd(l):
        def body(t, carry):
            col, pre, cdf, act = up_part(l, t)
            acc[EV] += mm(act, wd[l, pl.ds(col, DM), :])
            return carry

        acc[EV] = jnp.zeros_like(acc)
        lax.fori_loop(0, 4, body, 0)

    def mlp_a(l, dout):
        def body(t, carry):
            col, pre, cdf, act = up_part(l, t)
            act_s[:, pl.ds(col, DM)] = act
            slope_s[:, pl.ds(col, DM)] = cdf + pre * (0.3989422804014327 * jnp.exp(-0.5 * pre * pre))
            gt = mm_tn(act, dout[EV])
            for i in range(2):
                gd[lax.div(t, 2), lax.rem(t, 2), i] = gt[SEQ * i:SEQ * i + SEQ].reshape(2, LN, DM)
            return carry

        lax.fori_loop(0, 4, body, 0)

    def mlp_b(l, dout, fwd):
        def body(t, carry):
            col = pl.multiple_of(t * DM, DM)
            wd_t = wd[l, pl.ds(col, DM), :]
            if fwd:
                acc[EV] += mm(act_s[:, pl.ds(col, DM)], wd_t)
            dpre = mm_nt(dout[EV], wd_t).astype(BF).astype(F32) * slope_s[:, pl.ds(col, DM)]
            gub[0:1, pl.ds(col, DM)] = col_sum(dpre)
            dpb = dpre.astype(BF)
            gu[:, :, :, :, :, pl.ds(col, DM)] = mm(nmt[EV], dpb).reshape(2, 2, 2, 2, SH, DM)
            dnm[EV] += mm_nt(dpb, wu[l, :, pl.ds(col, DM)])
            return carry

        if fwd:
            acc[EV] = jnp.zeros_like(acc)
        dnm[EV] = jnp.zeros_like(dnm)
        lax.fori_loop(0, 4, body, 0)

    def attn_grads(l, dout):
        ga[:, :, :, :, :, Q3:] = mm_tn(ctx[EV], dout[EV]).reshape(2, 2, 2, 2, SH, DM)
        for t in (2, 0, 1):
            cols = slice(DM * t, DM * t + DM)
            ga[:, :, :, :, :, cols] = mm(nat[EV], dqkv[:, cols]).reshape(2, 2, 2, 2, SH, DM)

    def layer_end(h_ref, l, dout):
        dna = mm_nt(dqkv[EV], wa[l, :, 0:Q3]).astype(BF).astype(F32)
        dnm32 = dnm[EV].astype(BF).astype(F32)
        xhat, rstd = normed(h_ref[EV], l)
        d32 = dout[EV].astype(F32)
        gvec[0:1, :] = col_sum(dna * xhat)
        gvec[1:2, :] = col_sum(dna)
        gvec[2:3, :] = col_sum(d32)
        gvec[3:4, :] = col_sum(dnm32 * xhat)
        gvec[4:5, :] = col_sum(dnm32)
        gvec[5:6, :] = gvec[2:3, :]
        dx = dna * vec[l, 0:1, :] + dnm32 * vec[l, 3:4, :]
        dhid = rstd * (dx - row_of(jnp.mean, dx) - xhat * row_of(jnp.mean, dx * xhat))
        return (d32 + dhid).astype(BF)

    def small_grads(l):
        for d in range(ND):
            gs[l, d] = jnp.zeros((8, LN), F32)
            gs[l, d, 0:6, 0:SH] = gvec[0:6, SH * d:SH * d + SH]
            gs[l, d, 6:7, :] = gub[0:1, LN * d:LN * d + LN]
            for lo, col, n in bias_parts(d):
                gs[l, d, 7:8, lo:lo + n] = gqb[0:1, col:col + n]

    def bias_parts(d):
        base = HD * (d // 2)
        if d % 2 == 0:
            return ((0, base, HD), (HD, DM + base, SH))
        return ((0, DM + base + SH, SH), (SH, 1024 + base, HD))

    def peer(i):
        t = lax.rem(me + i, ND)
        return t, (lax.div(t, 8), lax.rem(t, 8))

    def small_send(l):
        def body(i, carry):
            t, to = peer(i)
            pltpu.make_async_remote_copy(src_ref=gs.at[l, t], dst_ref=gr.at[l, me], send_sem=gr_send.at[l],
                                         recv_sem=gr_recv.at[l], device_id=to, device_id_type=MESH).start()
            return carry
        lax.fori_loop(1, ND, body, 0)
        gr[l, me] = gs[l, me]

    def small_finish(l):
        whole = pltpu.make_async_remote_copy(src_ref=gs.at[l, pl.ds(0, ND - 1)], dst_ref=gr.at[l, pl.ds(0, ND - 1)],
                                             send_sem=gr_send.at[l], recv_sem=gr_recv.at[l],
                                             device_id=dev(chip, other), device_id_type=MESH)
        whole.wait_send()
        whole.wait_recv()
        total = gr[l, 0]
        for d in range(1, ND):
            total = total + gr[l, d]
        os_ref[l] = total

    native_in = pltpu.make_async_copy(wq_in, native, loc_sem.at[0, 0])
    first = [pltpu.make_async_copy(wu_in.at[0], block(0, UP, chip, core), loc_sem.at[0, 1])]
    qo = pl.ds(pl.multiple_of(me * SH, SH), SH)
    rest = [pltpu.make_async_copy(wo_in.at[l], W[AO].at[l, qo, pl.ds(Q3, DM)], loc_sem.at[l + 2, 2])
            for l in range(LAYERS)]
    rest += [pltpu.make_async_copy(wd_in.at[l], block(l, DN, chip, core), loc_sem.at[l + 2, 3]) for l in range(LAYERS)]
    rest += [pltpu.make_async_copy(wu_in.at[1], block(1, UP, chip, core), loc_sem.at[0, 2]),
             pltpu.make_async_copy(x_in, x_ref, loc_sem.at[0, 3]),
             pltpu.make_async_copy(cot_in, cot_ref, loc_sem.at[1, 0]),
             pltpu.make_async_copy(rope_in, rope_ref, loc_sem.at[1, 1])]
    params, tmp = (p0, p1, p2, p3, p4, p5, p6, p7), (v0, v1, v2, v3, v4, v5, v6, v7)
    little = [pltpu.make_async_copy(params[i], tmp[i], loc_sem.at[4 + i // 4, i % 4]) for i in range(8)]
    first[0].start()
    native_in.start()
    for cp in little + rest:
        cp.start()

    barrier = pltpu.get_barrier_semaphore()

    def greet(i, carry):
        pl.semaphore_signal(barrier, inc=1, device_id=peer(i)[1], device_id_type=MESH)
        return carry

    lax.fori_loop(1, ND, greet, 0)
    first[0].wait()
    pl.semaphore_wait(barrier, ND - 1)
    own(0, UP)

    native_in.wait()
    for l in range(LAYERS):
        flat = native[l].astype(F32).reshape(SEQ, 3 * HD)
        spread[0] = flat[:, :LN]
        spread[1, :, :HD] = flat[:, LN:]
        for h in range(8):
            rows = [spread[i, pl.ds(h, SH, stride=8), :].astype(BF) for i in range(2)]
            for t in range(3):
                lo = HD * (t % 2)
                wa[l, qo, DM * t + HD * h:DM * t + HD * h + HD] = rows[t // 2][:, lo:lo + HD]
        if l == 0:
            for cp in rest:
                cp.wait()
            own(0, AO)
    for i in range(8):
        little[i].wait()
        for l in range(LAYERS):
            smalls[me, l, i:i + 1, 0:tmp[i].shape[1]] = tmp[i][l:l + 1, :].astype(F32)

    def send_small(i, carry):
        pltpu.make_async_remote_copy(src_ref=smalls.at[me], dst_ref=smalls.at[me], send_sem=sm_send,
                                     recv_sem=sm_recv, device_id=peer(i)[1], device_id_type=MESH).start()
        return carry

    lax.fori_loop(1, ND, send_small, 0)
    f1(0, UP)
    f2(0, UP)
    own(0, DN)
    f1(0, AO)
    f3(0, UP)
    f2(0, AO)
    whole = pltpu.make_async_remote_copy(src_ref=smalls.at[pl.ds(0, ND - 1)], dst_ref=smalls.at[pl.ds(0, ND - 1)],
                                         send_sem=sm_send, recv_sem=sm_recv, device_id=dev(chip, other),
                                         device_id_type=MESH)
    whole.wait_send()
    whole.wait_recv()
    for l in range(LAYERS):
        for d in range(ND):
            vec[l, 0:6, SH * d:SH * d + SH] = smalls[d, l, 0:6, 0:SH]
            upb[l, 0:1, LN * d:LN * d + LN] = smalls[d, l, 6:7, :]
            for lo, col, n in bias_parts(d):
                qkvb[l, 0:1, col:col + n] = smalls[d, l, 7:8, lo:lo + n]
    norms(x_ref, 0, False)
    f1(0, DN)
    f3(0, AO)
    f4(0, UP)
    own(1, UP)
    f2(0, DN)
    f4(0, AO)
    got_partner(0, AO)
    make_qkv(0)
    f3(0, DN)
    f1(1, UP)
    heads(False, 0, 2)
    own(1, DN)
    heads(False, 2, 4)
    f2(1, UP)
    f3(1, UP)
    f1(1, DN)
    f4(0, DN)
    got_partner(0, UP)
    got_partner(0, DN)
    mlp_fwd(0)
    f2(1, DN)
    own(1, AO)
    acc[EV] += mm(ctx[EV], wa[0, :, Q3:])
    h1[EV] = (x_ref[EV].astype(F32) + acc[EV] + vec[0, 2:3, :] + vec[0, 5:6, :]).astype(BF)
    norms(h1, 1, True)
    f3(1, DN)
    f4(1, UP)
    got_partner(1, UP)
    f1(1, AO)
    f2(1, AO)
    mlp_a(1, cot_ref)
    s0(1, DN)
    f4(1, DN)
    s1(1, DN)
    f3(1, AO)
    got_partner(1, DN)
    mlp_b(1, cot_ref, True)
    s0(1, UP)
    s1(1, UP)
    f4(1, AO)
    got_partner(1, AO)
    make_qkv(1)
    dctx[EV] = mm_nt(cot_ref[EV], wa[1, :, Q3:]).astype(BF)
    heads(True, 0, 2)
    s2(1, DN)
    heads(True, 2, 4)
    attn_grads(1, cot_ref)
    s0(1, AO)
    s2(1, UP)
    acc[EV] += mm(ctx[EV], wa[1, :, Q3:])
    y_ref[EV] = (h1[EV].astype(F32) + acc[EV] + vec[1, 2:3, :] + vec[1, 5:6, :]).astype(BF)
    dh[EV] = layer_end(h1, 1, cot_ref)
    s1(1, AO)
    small_grads(1)
    small_send(1)

    norms(x_ref, 0, True)
    drained(1, DN, 0)
    drained(1, UP, 0)
    mlp_a(0, dh)
    s0(0, DN)
    s3(1, DN)
    s1(0, DN)
    mlp_b(0, dh, False)
    s0(0, UP)
    make_qkv(0)
    dctx[EV] = mm_nt(dh[EV], wa[0, :, Q3:]).astype(BF)
    s1(0, UP)
    heads(True, 0, 4)
    s2(1, AO)
    s3(1, UP)
    drained(1, AO, 0)
    attn_grads(0, dh)
    s0(0, AO)
    xg_ref[EV] = layer_end(x_ref, 0, dh)
    small_grads(0)
    small_send(0)
    s1(0, AO)
    for stage, l, w in ((s2, 0, DN), (s2, 0, UP), (s3, 1, AO), (s2, 0, AO), (s3, 0, DN), (s3, 0, UP), (s4, 1, DN),
                        (s4, 1, UP), (s4, 1, AO), (s3, 0, AO)):
        stage(l, w)
    small_finish(1)
    small_finish(0)
    for w in (DN, UP, AO):
        s4(0, w)
    for w in (DN, UP, AO):
        drained(0, w, 0)
        for l in range(LAYERS):
            sent(l, w)
            for stage in range(1, 4):
                drained(l, w, stage)


def finish(y, xg, oq, oo, ou, od, osm, *outs):
    *outs, spread = outs
    yo, xo, g1, b1, gq, bq, go, bo, g2, b2, gup, bu, gdn, bd = outs
    yo[0] = y[EV]
    xo[0] = xg[EV]
    go[EV] = oo[EV]
    gup[EV] = ou[EV]
    gdn[EV] = od[EV]
    for row, ref in enumerate((g1, b1, bo, g2, b2, bd, bu, bq)):
        for l in range(LAYERS):
            ref[l:l + 1, :] = osm[l, row:row + 1, 0:ref.shape[1]].astype(BF)
    for l in range(LAYERS):
        for h in range(8):
            q, k, v = (oq[l, :, DM * t + HD * h:DM * t + HD * h + HD].astype(F32) for t in range(3))
            spread[0, pl.ds(h, SH, stride=8), :] = jnp.concatenate([q, k], axis=1)
            spread[1, pl.ds(h, SH, stride=8), :] = jnp.concatenate([v, v], axis=1)
        gq[l, :, :, :LN] = spread[0].reshape(SH, 8, LN).astype(BF)
        gq[l, :, :, LN:] = spread[1, :, :HD].reshape(SH, 8, HD).astype(BF)


def rope_constants():
    rot, half, hd = 16, 8, HD
    inv = (1.0 / (10000.0 ** (np.arange(0, rot, 2, dtype=np.float32) / np.float32(rot)))).astype(np.float32)
    ang = np.arange(SEQ, dtype=np.float32)[:, None] * inv[None, :]
    cos, sin = np.cos(ang).astype(np.float32), np.sin(ang).astype(np.float32)
    c = np.ones((SEQ, LN), np.float32)
    p = np.zeros((SEQ, LN), np.float32)
    q = np.zeros((SEQ, LN), np.float32)
    for base in (0, hd):
        c[:, base:base + half] = cos
        c[:, base + half:base + rot] = cos
        p[:, base:base + half] = -sin
        q[:, base + half:base + rot] = sin
    return np.stack([c, p, q])


def solution(mesh):
    shard_axes = ('node', 'local')
    act_spec = P(shard_axes)
    param_spec = P(None, shard_axes)
    consts = rope_constants()
    vm = pl.BlockSpec(memory_space=pltpu.VMEM)
    hbm = pl.BlockSpec(memory_space=pl.ANY)

    def device_step(x, y_cot, g1, b1, wqkv, bqkv, wout, bout, g2, b2, wup, bup, wdn, bdn):
        little = (g1, b1, bout, g2, b2, bdn, bup, bqkv)

        def v(shape, dt):
            return pltpu.VMEM(shape, dt)

        wshape = [(LAYERS, ND * ROWS[w], COLS[w]) for w in range(3)]
        scratch = [v(wshape[w], BF) for w in range(3)]
        scratch += [v((2, 2, 2, 2, ROWS[w], COLS[w]), F32) for w in range(3)]
        for lead in ((2, 2, 2), (2, 2), (2,), ()):
            scratch += [v((LAYERS,) + lead + (ROWS[w], COLS[w]), F32) for w in range(3)]
        scratch += [v((ND, LAYERS, 8, LN), F32)] + [v(p.shape, BF) for p in little]
        scratch += [v((LAYERS, 8, DM), F32), v((LAYERS, 1, FF), F32),
                    v((LAYERS, 1, 3 * DM), F32), v((LAYERS, ND, 8, LN), F32), v((LAYERS, ND, 8, LN), F32),
                    v((8, DM), F32), v((1, FF), F32), v((1, 3 * DM), F32)]
        scratch += [v((SEQ, DM), BF), v((SEQ, DM), BF), v((3, SEQ, LN), F32), v((LAYERS, SH, 8, 3 * HD), BF),
                    v((2, SEQ, LN), F32), v((SEQ, FF), BF), v((SEQ, FF), F32)]
        scratch += [v((SEQ, DM), BF), v((SEQ, DM), BF), v((SEQ, DM), BF), v((SEQ, DM), BF),
                    v((DM, SEQ), BF), v((DM, SEQ), BF), v((SEQ, 3 * DM), BF), v((SEQ, 3 * DM), BF),
                    v((SEQ, DM), BF), v((SEQ, DM), BF), v((SEQ, DM), F32), v((SEQ, DM), F32)]
        dma = pltpu.SemaphoreType.DMA
        scratch += [dma((6, 4)), dma((LAYERS, 3)), dma((LAYERS, 3, 3, 8)), dma((LAYERS, 3)), dma((LAYERS, 3, 3, 4)),
                    dma((LAYERS, 3, 3, 4)), dma, dma, dma((LAYERS,)), dma((LAYERS,))]
        sds = jax.ShapeDtypeStruct
        mids = pl.pallas_call(
            kernel,
            out_shape=[sds((SEQ, DM), BF), sds((SEQ, DM), BF), sds((LAYERS, SH, Q3), BF), sds((LAYERS, SH, DM), BF),
                       sds((LAYERS, SH, FF), BF), sds((LAYERS, LN, DM), BF), sds((LAYERS, 8, LN), F32)],
            in_specs=[hbm] * 15,
            out_specs=[vm] * 7,
            scratch_shapes=scratch,
            compiler_params=pltpu.CompilerParams(has_side_effects=True, collective_id=0, vmem_limit_bytes=67043328),
            name='step',
        )(x[0], y_cot[0], wqkv, wout, wup, wdn, *little, consts)
        y, xg, oq, oo, ou, od, osm = mids
        like = (x, y_cot, g1, b1, wqkv, bqkv, wout, bout, g2, b2, wup, bup, wdn, bdn)
        return pl.pallas_call(finish, out_shape=[sds(p.shape, BF) for p in like], in_specs=[vm] * 7,
                              out_specs=[vm] * 14, scratch_shapes=[v((2, SEQ, LN), F32)],
                              name='finish')(y, xg, oq, oo, ou, od, osm)

    return jax.shard_map(device_step, mesh=mesh,
                         in_specs=(act_spec, act_spec) + (param_spec,) * 12,
                         out_specs=(act_spec, act_spec) + (param_spec,) * 12,
                         check_vma=False)
```

time: 183 us -> 141 us (0.77)
  Pallas kernels: 162 us -> 140 us
  local copies, waits for them, and re-layouts: 18.7 us -> 0 us
    pallas_call x1, Pallas kernels: 162 us -> 138 us  [device_step(): pl.pallas_call(kernel, out_shape=[sds((SEQ, DM), BF), sds((SEQ, DM), BF),...]
    unnamed x37 -> x0, local copies, waits for them, and re-layouts: 12.9 us -> none
    reshape x5 -> x0, local copies, waits for them, and re-layouts: 3.19 us -> none  [the longest x2 1.72 us: device_step(): wqkv.reshape(LAYERS, SH, 8, 3, HD).transpose(0, 1, 3, 2, 4)]
    pallas_call x0 -> x1, Pallas kernels: none -> 2.53 us  [device_step(): pl.pallas_call(finish, out_shape=[sds(p.shape, BF) for p in like], in_spe...]
    slice x5 -> x0, local copies, waits for them, and re-layouts: 2.43 us -> none  [the longest x1 1.47 us: device_step(): oa[:, :, Q3:]]
where the time goes in v3:
time: 141 us
  Pallas kernels  140 us (99%)
    pallas_call x1, Pallas kernels, device_step(): pl.pallas_call(kernel, out_shape=[sds((SEQ, DM), BF), sds((SEQ, DM), BF),...  138 us

profile of v3, /device:TPU:0, one launch (start us, length us, event | category | flops | bytes accessed | tf_op | source)
XLA Modules:
  0.0 140.9 jit_solution(2771545735510157865)
XLA Ops:
  0.7 137.7 %step.1 = (bf16[256,512]{1,0:T(8,128)(2,1)}, bf16[256,512]{1,0:T(8,128)(2,1)}, bf16[2,32,1536]{2,1,0:T(8,128)(2,1)}, bf16[2,32,512]{2,1,0:T(8,128)(2,1)}, bf16[2...) custom-call(bf16[256,512]{1,0:T(8,128)(2,1)} %bitcast.2, bf16[256,512]{1,0:T(8,128)(2,1)} %bitcast.3, ...), custom_call_target="tpu_custom_call" | custom-call | tf_op jit(solution)/shard_map/step/pallas_call | solution.py:627
  138.3 2.5 %finish.1 = (bf16[1,256,512]{2,1,0:T(8,128)(2,1)}, bf16[1,256,512]{2,1,0:T(8,128)(2,1)}, bf16[2,32]{1,0:T(2,128)(2,1)}, bf16[2,32]{1,0:T(2,128)(2,1)}, bf16[2,32...) custom-call(bf16[256,512]{1,0:T(8,128)(2,1)} %get-tuple-element.21.y, ...), custom_call_target="tpu_custom_call" | custom-call | tf_op jit(solution)/shard_map/finish/pallas_call | solution.py:639

commit v4 on v3

v4 whole, which is shorter than its diff:
```python
import numpy as np
import jax
import jax.numpy as jnp
from jax import lax
from jax.experimental import pallas as pl
from jax.experimental.pallas import tpu as pltpu
from jax.sharding import PartitionSpec as P

BF, F32 = jnp.bfloat16, jnp.float32
MESH = pl.DeviceIdType.MESH
EPSILON = 1e-5
LAYERS, SEQ, DM, FF, ND = 2, 256, 512, 2048, 16
SH, HD, LN, Q3 = 32, 64, 128, 1536
ROWS = (SH, SH, LN, 8)
COLS = (FF, FF, DM, LN)
WIDTH = FF + LN
AO, UP, DN, SM = range(4)
ORDERS = ((1, 2, 4), (2, 4, 1), (4, 1, 2))
CHIP_AXES = [4, 2, 1]
CUTS = ((0, 384, 1152, FF), (0, 384, 1152, FF), (0, SH, 80, LN))
WIDE = (0, 384, 1152, WIDTH)
ROUTES = ((1, 2), (2, 1))
ALL, EV = slice(None), ...
TOK = 2 * SEQ


def routes(w):
    return ORDERS[:1] if w == SM else ROUTES


def axes_of(w):
    return CHIP_AXES if w == SM else CHIP_AXES[1:]


def piece(w, k):
    if w == SM:
        return ALL, ALL
    n = (ROWS if w == DN else COLS)[w] // 2
    part = slice(n * k, n * k + n)
    return (part, ALL) if w == DN else (ALL, part)


def bit(v, a):
    return lax.rem(lax.div(v, a), 2)


def flip(v, mask):
    for a in (1, 2, 4):
        if mask & a:
            v = v + a - 2 * a * bit(v, a)
    return v


def col_sum(v):
    return jnp.sum(v, axis=0, keepdims=True)


def row_of(f, v):
    return f(v, axis=-1, keepdims=True)


def mm(a, b):
    return jnp.dot(a, b, preferred_element_type=F32)


def mm_nt(a, b):
    return lax.dot_general(a, b, (((1,), (1,)), ((), ())), preferred_element_type=F32)


def mm_tn(a, b):
    return lax.dot_general(a, b, (((0,), (0,)), ((), ())), preferred_element_type=F32)


def kernel(x_in, cot_in, wq_in, wo_in, wu_in, wd_in, p0, p1, p2, p3, p4, p5, p6, p7, rope_in,
           y_ref, xg_ref, oq_ref, oo_ref, ou_ref, od_ref, os_ref,
           wa, wu, wd, ga, gu, gd, gs, ra0, ra1, ra2, ru0, ru1, ru2, rd0, rd1, rd2, rs0, rs1, rs2, rs3,
           v0, v1, v2, v3, v4, v5, v6, v7, vec, upb, qkvb, gvec, gub, gqb,
           x_ref, cot_ref, rope_ref, native, spread, act_s, slope_s,
           h1, dh, na, nm, nat, nmt, qkv, dqkv, ctx, dctx, acc, dnm,
           loc_sem, ag_send, ag_ici, ag_d2d, rs_send, rs_recv, ex_send, ex_recv):
    me = lax.axis_index('node') * 8 + lax.axis_index('local')
    chip = lax.div(me, 2)
    core = lax.rem(me, 2)
    other = 1 - core
    W, G = (wa, wu, wd), (ga, gu, gd, gs)
    R = ((ra0, ra1, ra2), (ru0, ru1, ru2), (rd0, rd1, rd2), (rs0, rs1, rs2, rs3))
    node = lax.div(chip, 4)
    zrows = pl.ds(pl.multiple_of(node * SEQ, SEQ), SEQ)

    def dev(c, k):
        i = c * 2 + k
        return (lax.div(i, 8), lax.rem(i, 8))

    def rows_of(l, w, start, n):
        rows = pl.ds(start, n * ROWS[w])
        if w == AO and l == 1:
            return W[w].at[l, rows, pl.ds(0, FF)]
        return W[w].at[l, rows]

    def block(l, w, c, k):
        return rows_of(l, w, pl.multiple_of((c * 2 + k) * ROWS[w], ROWS[w]), 1)

    def part(l, w, k, mask):
        base = (flip(chip, mask) * 2 + core) * ROWS[w]
        cuts = WIDE if w == AO and l == 0 else CUTS[w]
        lo, hi = cuts[k], cuts[k + 1]
        if w == DN:
            return W[w].at[l, pl.ds(pl.multiple_of(base + lo, 16), hi - lo)]
        return W[w].at[l, pl.ds(pl.multiple_of(base, SH), SH), lo:hi]

    def push(l, w, src, to, recv_sem):
        pltpu.make_async_remote_copy(src_ref=src, dst_ref=src, send_sem=ag_send.at[l, w], recv_sem=recv_sem,
                                     device_id=to, device_id_type=MESH).start()

    def to_link(l, w, k, mask, a):
        push(l, w, part(l, w, k, mask), dev(flip(chip, a), core), ag_ici.at[l, w, k, mask ^ a])

    def to_partner(l, w, k, mask):
        push(l, w, part(l, w, k, mask), dev(chip, other), ag_d2d.at[l, w])

    def await_in(l, w, src, recv_sem):
        pltpu.make_async_remote_copy(src_ref=src, dst_ref=src, send_sem=ag_send.at[l, w], recv_sem=recv_sem,
                                     device_id=dev(chip, other), device_id_type=MESH).wait_recv()

    def got(l, w, k, mask):
        await_in(l, w, part(l, w, k, mask), ag_ici.at[l, w, k, mask])

    def got_partner(l, w):
        await_in(l, w, rows_of(l, w, 0, 8), ag_d2d.at[l, w])

    def sent(l, w):
        src = rows_of(l, w, 0, 15)
        pltpu.make_async_remote_copy(src_ref=src, dst_ref=src, send_sem=ag_send.at[l, w], recv_sem=ag_d2d.at[l, w],
                                     device_id=dev(chip, other), device_id_type=MESH).wait_send()

    def own(l, w):
        for i in range(3):
            for k in range(3):
                to_link(l, w, k, 0, ORDERS[k][i])
        push(l, w, block(l, w, chip, core), dev(chip, other), ag_d2d.at[l, w])

    def f1(l, w):
        for k, (a, b, c) in enumerate(ORDERS):
            got(l, w, k, a)
            to_link(l, w, k, a, b)
        for k, (a, b, c) in enumerate(ORDERS):
            to_link(l, w, k, a, c)
            to_partner(l, w, k, a)

    def f2(l, w):
        for k, (a, b, c) in enumerate(ORDERS):
            got(l, w, k, b)
            to_link(l, w, k, b, c)
            to_partner(l, w, k, b)

    def f3(l, w):
        for k, (a, b, c) in enumerate(ORDERS):
            got(l, w, k, a | b)
            to_link(l, w, k, a | b, c)
            to_partner(l, w, k, a | b)

    def f4(l, w):
        for i in range(4):
            for k, (a, b, c) in enumerate(ORDERS):
                m = (c, a | c, b | c, 7)[i]
                got(l, w, k, m)
                to_partner(l, w, k, m)

    rs = {}

    def rs_copy(l, w, k, stage, src, dst, to):
        cp = pltpu.make_async_remote_copy(src_ref=src, dst_ref=dst, send_sem=rs_send.at[l, w, k, stage],
                                          recv_sem=rs_recv.at[l, w, k, stage], device_id=to, device_id_type=MESH)
        cp.start()
        rs[l, w, k, stage] = cp

    def pick(axes, a, v):
        return tuple(v if m == a else ALL for m in axes)

    def drained(l, w, stage):
        for k in range(len(routes(w))):
            rs[l, w, k, stage].wait_send()

    def step(l, w, stage):
        axes = axes_of(w)
        n = len(axes)
        for k, route in enumerate(routes(w)):
            cut = piece(w, k)
            if stage == 0:
                rs_copy(l, w, k, 0, G[w].at[(ALL,) * n + (other,) + cut], R[w][0].at[(l,) + (ALL,) * n + cut],
                        dev(chip, other))
                continue
            rs[l, w, k, stage - 1].wait_recv()
            buf = R[w][stage - 1]
            left = [m for m in axes if m not in route[:stage - 1]]
            before = [m for m in axes if m not in route[:stage - 2]] if stage > 1 else axes

            def mine(where):
                if stage == 1:
                    return G[w][where + (core,) + cut]
                at = list(where)
                at.insert(before.index(route[stage - 2]), bit(chip, route[stage - 2]))
                return R[w][stage - 2][(l,) + tuple(at) + cut]

            if stage == n + 1:
                emit(l, w, k, cut, buf[(l,) + cut] + mine(()))
                continue
            for i in range(2 ** len(left)):
                where = tuple((i >> j) & 1 for j in range(len(left)))
                at = (l,) + where + cut
                buf[at] = buf[at] + mine(where)
            a = route[stage - 1]
            src = buf.at[(l,) + pick(left, a, 1 - bit(chip, a)) + cut]
            rs_copy(l, w, k, stage, src, R[w][stage].at[(l,) + (ALL,) * (len(left) - 1) + cut],
                    dev(flip(chip, a), core))

    def emit(l, w, k, cut, total):
        if w == SM:
            os_ref[l] = total
            return
        total = total.astype(BF)
        if w != AO:
            (None, ou_ref, od_ref)[w][(l,) + cut] = total
        elif k == 0:
            oq_ref[(l,) + cut] = total
        else:
            n = Q3 - cut[1].start
            oq_ref[l, :, cut[1].start:] = total[:, :n]
            oo_ref[l] = total[:, n:]

    def s0(l, w):
        step(l, w, 0)

    def s1(l, w):
        step(l, w, 1)

    def s2(l, w):
        step(l, w, 2)

    def s3(l, w):
        step(l, w, 3)

    def s4(l, w):
        step(l, w, 4)

    def normed(h_bf):
        h32 = h_bf.astype(F32)
        cen = h32 - row_of(jnp.mean, h32)
        rstd = lax.rsqrt(row_of(jnp.mean, cen * cen) + EPSILON)
        return cen * rstd, rstd

    def norms(h_ref, l, bwd):
        xhat, _ = normed(h_ref[EV])
        n1 = (xhat * vec[l, 0:1, :] + vec[l, 1:2, :]).astype(BF)
        n2 = (xhat * vec[l, 3:4, :] + vec[l, 4:5, :]).astype(BF)
        na[EV] = n1
        nm[EV] = n2
        if bwd:
            nat[EV] = n1.T
            nmt[EV] = n2.T

    def rope(xs, back, n):
        c, p, q = (rope_ref[t, :n] for t in range(3))
        if back:
            return xs * c + pltpu.roll(xs * p, 8, 1) + pltpu.roll(xs * q, 120, 1)
        return xs * c + pltpu.roll(xs, 120, 1) * p + pltpu.roll(xs, 8, 1) * q

    def make_qkv(l):
        for t in range(3):
            cols = slice(DM * t, DM * t + DM)
            raw = mm(na[EV], wa[l, :, cols]) + qkvb[l, :, cols]
            for s in range(4):
                part = raw[:, LN * s:LN * s + LN]
                if t < 2:
                    part = rope(part, False, TOK)
                qkv[:, DM * t + LN * s:DM * t + LN * s + LN] = part.astype(BF)

    def heads(bwd, lo, hi):
        lane = lax.broadcasted_iota(jnp.int32, (1, LN), 1)
        masks = [(lane < HD).astype(F32).astype(BF), (lane >= HD).astype(F32).astype(BF)]
        causal = (lax.broadcasted_iota(jnp.int32, (SEQ, SEQ), 0) >= lax.broadcasted_iota(jnp.int32, (SEQ, SEQ), 1))

        def body(j, carry):
            seq = lax.div(j, 4)
            rows = pl.ds(pl.multiple_of(seq * SEQ, SEQ), SEQ)
            col = pl.multiple_of((j - 4 * seq) * LN, LN)
            q, k, v = (qkv[rows, pl.ds(col + DM * t, LN)] for t in range(3))
            ctx_sum = jnp.zeros((SEQ, LN), F32)
            if bwd:
                dc = dctx[rows, pl.ds(col, LN)]
                dq = jnp.zeros((SEQ, LN), F32)
                dk = jnp.zeros((SEQ, LN), F32)
                dv = jnp.zeros((SEQ, LN), F32)
            for mask in masks:
                qm = q * mask
                sc = jnp.where(causal, mm_nt(qm, k) * 0.125, -1e30)
                e = jnp.exp(sc - row_of(jnp.max, sc))
                p = e / row_of(jnp.sum, e)
                pb = p.astype(BF)
                ctx_sum = ctx_sum + mm(pb, v * mask)
                if bwd:
                    dcm = dc * mask
                    dp = mm_nt(dcm, v).astype(BF).astype(F32)
                    dv = dv + mm_tn(pb, dcm)
                    ds = (p * (dp - row_of(jnp.sum, dp * p)) * 0.125).astype(BF)
                    dq = dq + mm(ds, k * mask)
                    dk = dk + mm_tn(ds, qm)
            ctx[rows, pl.ds(col, LN)] = ctx_sum.astype(BF)
            if bwd:
                for t, d in enumerate((dq, dk, dv)):
                    d = d.astype(BF).astype(F32)
                    if t < 2:
                        d = rope(d, True, SEQ)
                    gqb[seq, :, pl.ds(col + DM * t, LN)] = col_sum(d)
                    dqkv[rows, pl.ds(col + DM * t, LN)] = d.astype(BF)
            return carry

        lax.fori_loop(lo, hi, body, 0)

    def up_part(l, t):
        col = pl.multiple_of(t * DM, DM)
        pre = mm(nm[EV], wu[l, :, pl.ds(col, DM)]) + upb[l, :, pl.ds(col, DM)]
        cdf = 0.5 * (1.0 + lax.erf(pre * 0.7071067811865476))
        return col, pre, cdf, (pre * cdf).astype(BF)

    def mlp_fwd(l):
        def body(t, carry):
            col, pre, cdf, act = up_part(l, t)
            acc[EV] += mm(act, wd[l, pl.ds(col, DM), :])
            return carry

        acc[EV] = jnp.zeros_like(acc)
        lax.fori_loop(0, 4, body, 0)

    def mlp_a(l, dout):
        def body(t, carry):
            col, pre, cdf, act = up_part(l, t)
            act_s[:, pl.ds(col, DM)] = act
            slope_s[:, pl.ds(col, DM)] = cdf + pre * (0.3989422804014327 * jnp.exp(-0.5 * pre * pre))
            return carry

        def grad(t, carry):
            col = pl.multiple_of(node * 2 * DM + t * DM, DM)
            gd[t] = mm_tn(act_s[:, pl.ds(col, DM)], dout[EV]).reshape(2, 2, LN, DM)
            return carry

        lax.fori_loop(0, 4, body, 0)
        lax.fori_loop(0, 2, grad, 0)

    def mlp_b(l, dout, fwd):
        def body(t, carry):
            col = pl.multiple_of(t * DM, DM)
            wd_t = wd[l, pl.ds(col, DM), :]
            if fwd:
                acc[:SEQ] += mm(act_s[:SEQ, pl.ds(col, DM)], wd_t)
            dpre = mm_nt(dout[EV], wd_t).astype(BF).astype(F32) * slope_s[:, pl.ds(col, DM)]
            gub[0:1, pl.ds(col, DM)] = col_sum(dpre[:SEQ])
            dpb = dpre.astype(BF)
            gu[:, :, :, :, pl.ds(col, DM)] = mm(nmt[zrows, :], dpb).reshape(2, 2, 2, SH, DM)
            dnm[EV] += mm_nt(dpb, wu[l, :, pl.ds(col, DM)])
            return carry

        if fwd:
            acc[EV] = jnp.zeros_like(acc)
        dnm[EV] = jnp.zeros_like(dnm)
        lax.fori_loop(0, 4, body, 0)

    def attn_grads(l, dout):
        ga[:, :, :, :, Q3:] = mm_tn(ctx[:, zrows], dout[EV]).reshape(2, 2, 2, SH, DM)
        for t in range(3):
            cols = slice(DM * t, DM * t + DM)
            ga[:, :, :, :, cols] = mm(nat[zrows, :], dqkv[:, cols]).reshape(2, 2, 2, SH, DM)

    def layer_end(h_ref, l, dout, n):
        dna = mm_nt(dqkv[:n], wa[l, :, 0:Q3]).astype(BF).astype(F32)
        dnm32 = dnm[:n].astype(BF).astype(F32)
        xhat, rstd = normed(h_ref[:n])
        d32 = dout[:n].astype(F32)
        own_tok = slice(0, SEQ)
        sums = [dna * xhat, dna, d32, dnm32 * xhat, dnm32, d32]
        for i, v in enumerate(sums):
            gvec[i:i + 1, :] = col_sum(v[own_tok])
        dx = dna * vec[l, 0:1, :] + dnm32 * vec[l, 3:4, :]
        dhid = rstd * (dx - row_of(jnp.mean, dx) - xhat * row_of(jnp.mean, dx * xhat))
        return (d32 + dhid).astype(BF)

    def small_grads():
        for d in range(ND):
            at = (d // 8, d // 4 % 2, d // 2 % 2, d % 2)
            gs[at] = jnp.zeros((8, LN), F32)
            gs[at + (slice(0, 6), slice(0, SH))] = gvec[0:6, SH * d:SH * d + SH]
            gs[at + (slice(6, 7), ALL)] = gub[0:1, LN * d:LN * d + LN]
            for lo, col, n in bias_parts(d):
                gs[at + (slice(7, 8), slice(lo, lo + n))] = gqb[0, :, col:col + n]

    def vectors():
        for d in range(ND):
            both = wa[0, SH * d:SH * d + 16, FF:].astype(F32)
            for l in range(LAYERS):
                rows = both[8 * l:8 * l + 8]
                vec[l, 0:6, SH * d:SH * d + SH] = rows[0:6, 0:SH]
                upb[l, 0:1, LN * d:LN * d + LN] = rows[6:7]
                for lo, col, n in bias_parts(d):
                    qkvb[l, 0:1, col:col + n] = rows[7:8, lo:lo + n]

    def bias_parts(d):
        base = HD * (d // 2)
        if d % 2 == 0:
            return ((0, base, HD), (HD, DM + base, SH))
        return ((0, DM + base + SH, SH), (SH, 1024 + base, HD))

    def swap(i, ref):
        return pltpu.make_async_remote_copy(src_ref=ref.at[pl.ds(0, SEQ)], dst_ref=ref.at[pl.ds(SEQ, SEQ)],
                                            send_sem=ex_send.at[i], recv_sem=ex_recv.at[i],
                                            device_id=dev(flip(chip, 4), core), device_id_type=MESH)

    swap_x, swap_cot = swap(0, x_ref), swap(1, cot_ref)
    native_in = pltpu.make_async_copy(wq_in, native, loc_sem.at[0, 0])
    first = [pltpu.make_async_copy(wu_in.at[0], block(0, UP, chip, core), loc_sem.at[0, 1])]
    qo = pl.ds(pl.multiple_of(me * SH, SH), SH)
    rest = [pltpu.make_async_copy(wo_in.at[l], W[AO].at[l, qo, pl.ds(Q3, DM)], loc_sem.at[l + 2, 2])
            for l in range(LAYERS)]
    rest += [pltpu.make_async_copy(wd_in.at[l], block(l, DN, chip, core), loc_sem.at[l + 2, 3]) for l in range(LAYERS)]
    rest += [pltpu.make_async_copy(wu_in.at[1], block(1, UP, chip, core), loc_sem.at[0, 2]),
             pltpu.make_async_copy(x_in, x_ref.at[pl.ds(0, SEQ)], loc_sem.at[0, 3]),
             pltpu.make_async_copy(cot_in, cot_ref.at[pl.ds(0, SEQ)], loc_sem.at[1, 0]),
             pltpu.make_async_copy(rope_in, rope_ref, loc_sem.at[1, 1])]
    params, tmp = (p0, p1, p2, p3, p4, p5, p6, p7), (v0, v1, v2, v3, v4, v5, v6, v7)
    little = [pltpu.make_async_copy(params[i], tmp[i], loc_sem.at[4 + i // 4, i % 4]) for i in range(8)]
    first[0].start()
    native_in.start()
    for cp in little + rest:
        cp.start()

    barrier = pltpu.get_barrier_semaphore()
    near = [dev(chip, other)] + [dev(flip(chip, a), core) for a in CHIP_AXES]
    for to in near:
        pl.semaphore_signal(barrier, inc=1, device_id=to, device_id_type=MESH)
    first[0].wait()
    pl.semaphore_wait(barrier, len(near))
    own(0, UP)

    native_in.wait()
    for l in range(LAYERS):
        flat = native[l].astype(F32).reshape(SEQ, 3 * HD)
        spread[0] = flat[:, :LN]
        spread[1, :, :HD] = flat[:, LN:]
        for h in range(8):
            rows = [spread[i, pl.ds(h, SH, stride=8), :].astype(BF) for i in range(2)]
            for t in range(3):
                lo = HD * (t % 2)
                wa[l, qo, DM * t + HD * h:DM * t + HD * h + HD] = rows[t // 2][:, lo:lo + HD]
        if l == 0:
            for cp in little + rest:
                cp.wait()
            spread[0, 0:SH] = jnp.zeros((SH, LN), F32)
            for i in range(8):
                for m in range(LAYERS):
                    spread[0, 8 * m + i:8 * m + i + 1, 0:tmp[i].shape[1]] = tmp[i][m:m + 1, :].astype(F32)
            wa[0, qo, FF:] = spread[0, 0:SH].astype(BF)
            own(0, AO)
    swap_x.start()
    f1(0, UP)
    f2(0, UP)
    own(0, DN)
    f1(0, AO)
    f3(0, UP)
    f2(0, AO)
    f1(0, DN)
    f3(0, AO)
    f4(0, UP)
    own(1, UP)
    f2(0, DN)
    swap_cot.start()
    f4(0, AO)
    got_partner(0, AO)
    vectors()
    swap_x.wait_recv()
    norms(x_ref, 0, False)
    make_qkv(0)
    f3(0, DN)
    f1(1, UP)
    heads(False, 0, 2)
    own(1, DN)
    heads(False, 2, 4)
    f2(1, UP)
    heads(False, 4, 6)
    f3(1, UP)
    f4(0, DN)
    heads(False, 6, 8)
    f1(1, DN)
    got_partner(0, UP)
    got_partner(0, DN)
    mlp_fwd(0)
    f2(1, DN)
    own(1, AO)
    acc[EV] += mm(ctx[EV], wa[0, :, Q3:FF])
    h1[EV] = (x_ref[EV].astype(F32) + acc[EV] + vec[0, 2:3, :] + vec[0, 5:6, :]).astype(BF)
    f3(1, DN)
    f4(1, UP)
    norms(h1, 1, True)
    f1(1, AO)
    f2(1, AO)
    got_partner(1, UP)
    swap_cot.wait_recv()
    mlp_a(1, cot_ref)
    s0(1, DN)
    f4(1, DN)
    s1(1, DN)
    f3(1, AO)
    got_partner(1, DN)
    mlp_b(1, cot_ref, True)
    s0(1, UP)
    f4(1, AO)
    s1(1, UP)
    got_partner(1, AO)
    make_qkv(1)
    dctx[EV] = mm_nt(cot_ref[EV], wa[1, :, Q3:FF]).astype(BF)
    heads(True, 0, 4)
    s2(1, DN)
    heads(True, 4, 8)
    attn_grads(1, cot_ref)
    s0(1, AO)
    s2(1, UP)
    acc[:SEQ] += mm(ctx[:SEQ], wa[1, :, Q3:FF])
    y_ref[EV] = (h1[:SEQ].astype(F32) + acc[:SEQ] + vec[1, 2:3, :] + vec[1, 5:6, :]).astype(BF)
    dh[EV] = layer_end(h1, 1, cot_ref, TOK)
    s1(1, AO)
    small_grads()
    s0(1, SM)

    norms(x_ref, 0, True)
    drained(1, DN, 0)
    drained(1, UP, 0)
    mlp_a(0, dh)
    s0(0, DN)
    s1(1, SM)
    s1(0, DN)
    mlp_b(0, dh, False)
    s0(0, UP)
    s2(1, AO)
    make_qkv(0)
    dctx[EV] = mm_nt(dh[EV], wa[0, :, Q3:FF]).astype(BF)
    s1(0, UP)
    heads(True, 0, 4)
    s2(0, DN)
    s2(1, SM)
    heads(True, 4, 8)
    drained(1, SM, 0)
    drained(1, AO, 0)
    attn_grads(0, dh)
    s0(0, AO)
    s3(1, SM)
    xg_ref[EV] = layer_end(x_ref, 0, dh, SEQ)
    s1(0, AO)
    small_grads()
    s0(0, SM)
    s2(0, UP)
    s1(0, SM)
    for stage, l, w in ((s3, 1, DN), (s3, 1, UP), (s3, 1, AO), (s4, 1, SM), (s2, 0, SM), (s3, 0, DN), (s2, 0, AO),
                        (s3, 0, UP), (s3, 0, SM), (s4, 0, SM), (s3, 0, AO)):
        stage(l, w)
    swap_x.wait_send()
    swap_cot.wait_send()
    for w in (DN, UP, AO, SM):
        drained(0, w, 0)
        for l in range(LAYERS):
            if w != SM:
                sent(l, w)
            for stage in range(1, len(axes_of(w)) + 1):
                drained(l, w, stage)


def finish(y, xg, oq, oo, ou, od, osm, *outs):
    *outs, spread = outs
    yo, xo, g1, b1, gq, bq, go, bo, g2, b2, gup, bu, gdn, bd = outs
    yo[0] = y[EV]
    xo[0] = xg[EV]
    go[EV] = oo[EV]
    gup[EV] = ou[EV]
    gdn[EV] = od[EV]
    for row, ref in enumerate((g1, b1, bo, g2, b2, bd, bu, bq)):
        for l in range(LAYERS):
            ref[l:l + 1, :] = osm[l, row:row + 1, 0:ref.shape[1]].astype(BF)
    for l in range(LAYERS):
        for h in range(8):
            q, k, v = (oq[l, :, DM * t + HD * h:DM * t + HD * h + HD].astype(F32) for t in range(3))
            spread[0, pl.ds(h, SH, stride=8), :] = jnp.concatenate([q, k], axis=1)
            spread[1, pl.ds(h, SH, stride=8), :] = jnp.concatenate([v, v], axis=1)
        gq[l, :, :, :LN] = spread[0].reshape(SH, 8, LN).astype(BF)
        gq[l, :, :, LN:] = spread[1, :, :HD].reshape(SH, 8, HD).astype(BF)


def rope_constants():
    rot, half, hd = 16, 8, HD
    inv = (1.0 / (10000.0 ** (np.arange(0, rot, 2, dtype=np.float32) / np.float32(rot)))).astype(np.float32)
    ang = np.arange(SEQ, dtype=np.float32)[:, None] * inv[None, :]
    cos, sin = np.cos(ang).astype(np.float32), np.sin(ang).astype(np.float32)
    c = np.ones((SEQ, LN), np.float32)
    p = np.zeros((SEQ, LN), np.float32)
    q = np.zeros((SEQ, LN), np.float32)
    for base in (0, hd):
        c[:, base:base + half] = cos
        c[:, base + half:base + rot] = cos
        p[:, base:base + half] = -sin
        q[:, base + half:base + rot] = sin
    return np.tile(np.stack([c, p, q]), (1, 2, 1))


def solution(mesh):
    shard_axes = ('node', 'local')
    act_spec = P(shard_axes)
    param_spec = P(None, shard_axes)
    consts = rope_constants()
    vm = pl.BlockSpec(memory_space=pltpu.VMEM)
    hbm = pl.BlockSpec(memory_space=pl.ANY)

    def device_step(x, y_cot, g1, b1, wqkv, bqkv, wout, bout, g2, b2, wup, bup, wdn, bdn):
        little = (g1, b1, bout, g2, b2, bdn, bup, bqkv)

        def v(shape, dt):
            return pltpu.VMEM(shape, dt)

        wshape = [(LAYERS, ND * ROWS[w], WIDTH if w == AO else COLS[w]) for w in range(3)]
        scratch = [v(wshape[w], BF) for w in range(3)]
        scratch += [v((2,) * (len(axes_of(w)) + 1) + (ROWS[w], COLS[w]), F32) for w in range(4)]
        for w in range(4):
            n = len(axes_of(w))
            scratch += [v((LAYERS,) + (2,) * (n - i) + (ROWS[w], COLS[w]), F32) for i in range(n + 1)]
        scratch += [v(p.shape, BF) for p in little]
        scratch += [v((LAYERS, 8, DM), F32), v((LAYERS, 1, FF), F32), v((LAYERS, 1, Q3), F32),
                    v((8, DM), F32), v((1, FF), F32), v((2, 1, Q3), F32)]
        scratch += [v((TOK, DM), BF)] * 2
        scratch += [v((3, TOK, LN), F32), v((LAYERS, SH, 8, 3 * HD), BF), v((2, SEQ, LN), F32), v((TOK, FF), BF),
                    v((TOK, FF), F32)]
        scratch += [v((TOK, DM), BF)] * 4 + [v((DM, TOK), BF)] * 2 + [v((TOK, Q3), BF)] * 2
        scratch += [v((TOK, DM), BF)] * 2 + [v((TOK, DM), F32)] * 2
        dma = pltpu.SemaphoreType.DMA
        scratch += [dma((6, 4)), dma((LAYERS, 3)), dma((LAYERS, 3, 3, 8)), dma((LAYERS, 3)), dma((LAYERS, 4, 3, 4)),
                    dma((LAYERS, 4, 3, 4)), dma((2,)), dma((2,))]
        sds = jax.ShapeDtypeStruct
        mids = pl.pallas_call(
            kernel,
            out_shape=[sds((SEQ, DM), BF), sds((SEQ, DM), BF), sds((LAYERS, SH, Q3), BF), sds((LAYERS, SH, DM), BF),
                       sds((LAYERS, SH, FF), BF), sds((LAYERS, LN, DM), BF), sds((LAYERS, 8, LN), F32)],
            in_specs=[hbm] * 15,
            out_specs=[vm] * 7,
            scratch_shapes=scratch,
            compiler_params=pltpu.CompilerParams(has_side_effects=True, collective_id=0, vmem_limit_bytes=67043328),
            name='step',
        )(x[0], y_cot[0], wqkv, wout, wup, wdn, *little, consts)
        y, xg, oq, oo, ou, od, osm = mids
        like = (x, y_cot, g1, b1, wqkv, bqkv, wout, bout, g2, b2, wup, bup, wdn, bdn)
        return pl.pallas_call(finish, out_shape=[sds(p.shape, BF) for p in like], in_specs=[vm] * 7,
                              out_specs=[vm] * 14, scratch_shapes=[v((2, SEQ, LN), F32)],
                              name='finish')(y, xg, oq, oo, ou, od, osm)

    return jax.shard_map(device_step, mesh=mesh,
                         in_specs=(act_spec, act_spec) + (param_spec,) * 12,
                         out_specs=(act_spec, act_spec) + (param_spec,) * 12,
                         check_vma=False)
```

time: 141 us -> 131 us (0.929)
  Pallas kernels: 140 us -> 130 us
    pallas_call x1, Pallas kernels: 138 us -> 128 us  [device_step(): pl.pallas_call(kernel, out_shape=[sds((SEQ, DM), BF), sds((SEQ, DM), BF),...]
where the time goes in v4:
time: 131 us
  Pallas kernels  130 us (99%)
    pallas_call x1, Pallas kernels, device_step(): pl.pallas_call(kernel, out_shape=[sds((SEQ, DM), BF), sds((SEQ, DM), BF),...  128 us

profile of v4, /device:TPU:0, one launch (start us, length us, event | category | flops | bytes accessed | tf_op | source)
XLA Modules:
  0.0 131.2 jit_solution(1282660748939480642)
XLA Ops:
  0.7 127.8 %step.1 = (bf16[256,512]{1,0:T(8,128)(2,1)}, bf16[256,512]{1,0:T(8,128)(2,1)}, bf16[2,32,1536]{2,1,0:T(8,128)(2,1)}, bf16[2,32,512]{2,1,0:T(8,128)(2,1)}, bf16[2...) custom-call(bf16[256,512]{1,0:T(8,128)(2,1)} %bitcast.2, bf16[256,512]{1,0:T(8,128)(2,1)} %bitcast.3, ...), custom_call_target="tpu_custom_call" | custom-call | tf_op jit(solution)/shard_map/step/pallas_call | solution.py:642
  128.5 2.5 %finish.1 = (bf16[1,256,512]{2,1,0:T(8,128)(2,1)}, bf16[1,256,512]{2,1,0:T(8,128)(2,1)}, bf16[2,32]{1,0:T(2,128)(2,1)}, bf16[2,32]{1,0:T(2,128)(2,1)}, bf16[2,32...) custom-call(bf16[256,512]{1,0:T(8,128)(2,1)} %get-tuple-element.21.y, ...), custom_call_target="tpu_custom_call" | custom-call | tf_op jit(solution)/shard_map/finish/pallas_call | solution.py:654

commit v5 on v4

--- a/solution.py
+++ b/solution.py
@@ -249,15 +249,14 @@
         rstd = lax.rsqrt(row_of(jnp.mean, cen * cen) + EPSILON)
         return cen * rstd, rstd
 
-    def norms(h_ref, l, bwd):
+    def norms(h_ref, l):
         xhat, _ = normed(h_ref[EV])
         n1 = (xhat * vec[l, 0:1, :] + vec[l, 1:2, :]).astype(BF)
         n2 = (xhat * vec[l, 3:4, :] + vec[l, 4:5, :]).astype(BF)
         na[EV] = n1
         nm[EV] = n2
-        if bwd:
-            nat[EV] = n1.T
-            nmt[EV] = n2.T
+        nat[l] = n1.T
+        nmt[l] = n2.T
 
     def rope(xs, back, n):
         c, p, q = (rope_ref[t, :n] for t in range(3))
@@ -273,46 +272,48 @@
                 part = raw[:, LN * s:LN * s + LN]
                 if t < 2:
                     part = rope(part, False, TOK)
-                qkv[:, DM * t + LN * s:DM * t + LN * s + LN] = part.astype(BF)
-
-    def heads(bwd, lo, hi):
+                qkv[l, :, DM * t + LN * s:DM * t + LN * s + LN] = part.astype(BF)
+
+    def heads(l, bwd, lo, hi):
         lane = lax.broadcasted_iota(jnp.int32, (1, LN), 1)
-        masks = [(lane < HD).astype(F32).astype(BF), (lane >= HD).astype(F32).astype(BF)]
-        causal = (lax.broadcasted_iota(jnp.int32, (SEQ, SEQ), 0) >= lax.broadcasted_iota(jnp.int32, (SEQ, SEQ), 1))
-
-        def body(j, carry):
-            seq = lax.div(j, 4)
-            rows = pl.ds(pl.multiple_of(seq * SEQ, SEQ), SEQ)
-            col = pl.multiple_of((j - 4 * seq) * LN, LN)
-            q, k, v = (qkv[rows, pl.ds(col + DM * t, LN)] for t in range(3))
-            ctx_sum = jnp.zeros((SEQ, LN), F32)
-            if bwd:
-                dc = dctx[rows, pl.ds(col, LN)]
-                dq = jnp.zeros((SEQ, LN), F32)
-                dk = jnp.zeros((SEQ, LN), F32)
-                dv = jnp.zeros((SEQ, LN), F32)
-            for mask in masks:
-                qm = q * mask
-                sc = jnp.where(causal, mm_nt(qm, k) * 0.125, -1e30)
+        sides = [(lane < HD).astype(F32), (lane >= HD).astype(F32)]
+        row, key = (lax.broadcasted_iota(jnp.int32, (SEQ, SEQ), t) for t in range(2))
+        causal = row >= key
+
+        def pair(seq, col):
+            rows = slice(SEQ * seq, SEQ * seq + SEQ)
+            q, k, v = (qkv[l, rows, pl.ds(col + DM * t, LN)] for t in range(3))
+            dc = dctx[rows, pl.ds(col, LN)] if bwd else None
+            out = dq = dk = dv = 0.0
+            for side in sides:
+                one, eighth = side.astype(BF), (side * 0.125).astype(BF)
+                qm = q * eighth
+                sc = jnp.where(causal, mm_nt(qm, k), -1e30)
                 e = jnp.exp(sc - row_of(jnp.max, sc))
-                p = e / row_of(jnp.sum, e)
+                p = e * (1.0 / row_of(jnp.sum, e))
                 pb = p.astype(BF)
-                ctx_sum = ctx_sum + mm(pb, v * mask)
+                out += mm(pb, v * one)
                 if bwd:
-                    dcm = dc * mask
+                    dcm = dc * one
                     dp = mm_nt(dcm, v).astype(BF).astype(F32)
-                    dv = dv + mm_tn(pb, dcm)
-                    ds = (p * (dp - row_of(jnp.sum, dp * p)) * 0.125).astype(BF)
-                    dq = dq + mm(ds, k * mask)
-                    dk = dk + mm_tn(ds, qm)
-            ctx[rows, pl.ds(col, LN)] = ctx_sum.astype(BF)
+                    ds = (p * (dp - row_of(jnp.sum, dp * p))).astype(BF)
+                    dq += mm(ds, k * eighth)
+                    dk += mm_tn(ds, qm)
+                    dv += mm_tn(pb, dcm)
+            ctx[rows, pl.ds(col, LN)] = out.astype(BF)
             if bwd:
                 for t, d in enumerate((dq, dk, dv)):
                     d = d.astype(BF).astype(F32)
                     if t < 2:
                         d = rope(d, True, SEQ)
-                    gqb[seq, :, pl.ds(col + DM * t, LN)] = col_sum(d)
+                    if seq == 0:
+                        gqb[0:1, pl.ds(col + DM * t, LN)] = col_sum(d)
                     dqkv[rows, pl.ds(col + DM * t, LN)] = d.astype(BF)
+
+        def body(j, carry):
+            col = pl.multiple_of(j * LN, LN)
+            for seq in range(2):
+                pair(seq, col)
             return carry
 
         lax.fori_loop(lo, hi, body, 0)
@@ -323,53 +324,51 @@
         cdf = 0.5 * (1.0 + lax.erf(pre * 0.7071067811865476))
         return col, pre, cdf, (pre * cdf).astype(BF)
 
-    def mlp_fwd(l):
+    def activate(l, fwd, lo, hi):
         def body(t, carry):
             col, pre, cdf, act = up_part(l, t)
-            acc[EV] += mm(act, wd[l, pl.ds(col, DM), :])
+            act_s[l, :, pl.ds(col, DM)] = act
+            slope_s[l, :, pl.ds(col, DM)] = cdf + pre * (0.3989422804014327 * jnp.exp(-0.5 * pre * pre))
+            if fwd:
+                acc[EV] += mm(act, wd[l, pl.ds(col, DM), :])
             return carry
 
-        acc[EV] = jnp.zeros_like(acc)
-        lax.fori_loop(0, 4, body, 0)
-
-    def mlp_a(l, dout):
-        def body(t, carry):
-            col, pre, cdf, act = up_part(l, t)
-            act_s[:, pl.ds(col, DM)] = act
-            slope_s[:, pl.ds(col, DM)] = cdf + pre * (0.3989422804014327 * jnp.exp(-0.5 * pre * pre))
-            return carry
-
+        if fwd and lo == 0:
+            acc[EV] = jnp.zeros_like(acc)
+        lax.fori_loop(lo, hi, body, 0)
+
+    def down_grad(l, dout):
         def grad(t, carry):
             col = pl.multiple_of(node * 2 * DM + t * DM, DM)
-            gd[t] = mm_tn(act_s[:, pl.ds(col, DM)], dout[EV]).reshape(2, 2, LN, DM)
+            gd[t] = mm_tn(act_s[l, :, pl.ds(col, DM)], dout[EV]).reshape(2, 2, LN, DM)
             return carry
 
-        lax.fori_loop(0, 4, body, 0)
         lax.fori_loop(0, 2, grad, 0)
 
-    def mlp_b(l, dout, fwd):
+    def mlp_b(l, dout, fwd, lo, hi):
         def body(t, carry):
             col = pl.multiple_of(t * DM, DM)
             wd_t = wd[l, pl.ds(col, DM), :]
             if fwd:
-                acc[:SEQ] += mm(act_s[:SEQ, pl.ds(col, DM)], wd_t)
-            dpre = mm_nt(dout[EV], wd_t).astype(BF).astype(F32) * slope_s[:, pl.ds(col, DM)]
+                acc[:SEQ] += mm(act_s[l, :SEQ, pl.ds(col, DM)], wd_t)
+            dpre = mm_nt(dout[EV], wd_t).astype(BF).astype(F32) * slope_s[l, :, pl.ds(col, DM)]
             gub[0:1, pl.ds(col, DM)] = col_sum(dpre[:SEQ])
             dpb = dpre.astype(BF)
-            gu[:, :, :, :, pl.ds(col, DM)] = mm(nmt[zrows, :], dpb).reshape(2, 2, 2, SH, DM)
+            gu[:, :, :, :, pl.ds(col, DM)] = mm(nmt[l, zrows, :], dpb).reshape(2, 2, 2, SH, DM)
             dnm[EV] += mm_nt(dpb, wu[l, :, pl.ds(col, DM)])
             return carry
 
-        if fwd:
-            acc[EV] = jnp.zeros_like(acc)
-        dnm[EV] = jnp.zeros_like(dnm)
-        lax.fori_loop(0, 4, body, 0)
+        if lo == 0:
+            dnm[EV] = jnp.zeros_like(dnm)
+            if fwd:
+                acc[EV] = jnp.zeros_like(acc)
+        lax.fori_loop(lo, hi, body, 0)
 
     def attn_grads(l, dout):
         ga[:, :, :, :, Q3:] = mm_tn(ctx[:, zrows], dout[EV]).reshape(2, 2, 2, SH, DM)
         for t in range(3):
             cols = slice(DM * t, DM * t + DM)
-            ga[:, :, :, :, cols] = mm(nat[zrows, :], dqkv[:, cols]).reshape(2, 2, 2, SH, DM)
+            ga[:, :, :, :, cols] = mm(nat[l, zrows, :], dqkv[:, cols]).reshape(2, 2, 2, SH, DM)
 
     def layer_end(h_ref, l, dout, n):
         dna = mm_nt(dqkv[:n], wa[l, :, 0:Q3]).astype(BF).astype(F32)
@@ -391,7 +390,7 @@
             gs[at + (slice(0, 6), slice(0, SH))] = gvec[0:6, SH * d:SH * d + SH]
             gs[at + (slice(6, 7), ALL)] = gub[0:1, LN * d:LN * d + LN]
             for lo, col, n in bias_parts(d):
-                gs[at + (slice(7, 8), slice(lo, lo + n))] = gqb[0, :, col:col + n]
+                gs[at + (slice(7, 8), slice(lo, lo + n))] = gqb[0:1, col:col + n]
 
     def vectors():
         for d in range(ND):
@@ -415,6 +414,7 @@
                                             device_id=dev(flip(chip, 4), core), device_id_type=MESH)
 
     swap_x, swap_cot = swap(0, x_ref), swap(1, cot_ref)
+    (A0, U0, D0, V0), (A1, U1, D1, V1) = [[(l, w) for w in (AO, UP, DN, SM)] for l in range(LAYERS)]
     native_in = pltpu.make_async_copy(wq_in, native, loc_sem.at[0, 0])
     first = [pltpu.make_async_copy(wu_in.at[0], block(0, UP, chip, core), loc_sem.at[0, 1])]
     qo = pl.ds(pl.multiple_of(me * SH, SH), SH)
@@ -424,7 +424,8 @@
     rest += [pltpu.make_async_copy(wu_in.at[1], block(1, UP, chip, core), loc_sem.at[0, 2]),
              pltpu.make_async_copy(x_in, x_ref.at[pl.ds(0, SEQ)], loc_sem.at[0, 3]),
              pltpu.make_async_copy(cot_in, cot_ref.at[pl.ds(0, SEQ)], loc_sem.at[1, 0]),
-             pltpu.make_async_copy(rope_in, rope_ref, loc_sem.at[1, 1])]
+             pltpu.make_async_copy(rope_in, rope_ref.at[:, pl.ds(0, SEQ)], loc_sem.at[1, 1]),
+             pltpu.make_async_copy(rope_in, rope_ref.at[:, pl.ds(SEQ, SEQ)], loc_sem.at[1, 2])]
     params, tmp = (p0, p1, p2, p3, p4, p5, p6, p7), (v0, v1, v2, v3, v4, v5, v6, v7)
     little = [pltpu.make_async_copy(params[i], tmp[i], loc_sem.at[4 + i // 4, i % 4]) for i in range(8)]
     first[0].start()
@@ -438,7 +439,7 @@
         pl.semaphore_signal(barrier, inc=1, device_id=to, device_id_type=MESH)
     first[0].wait()
     pl.semaphore_wait(barrier, len(near))
-    own(0, UP)
+    own(*U0)
 
     native_in.wait()
     for l in range(LAYERS):
@@ -458,108 +459,109 @@
                 for m in range(LAYERS):
                     spread[0, 8 * m + i:8 * m + i + 1, 0:tmp[i].shape[1]] = tmp[i][m:m + 1, :].astype(F32)
             wa[0, qo, FF:] = spread[0, 0:SH].astype(BF)
-            own(0, AO)
+            own(*A0)
     swap_x.start()
-    f1(0, UP)
-    f2(0, UP)
-    own(0, DN)
-    f1(0, AO)
-    f3(0, UP)
-    f2(0, AO)
-    f1(0, DN)
-    f3(0, AO)
-    f4(0, UP)
-    own(1, UP)
-    f2(0, DN)
-    swap_cot.start()
-    f4(0, AO)
-    got_partner(0, AO)
+    f1(*A0)
+    f1(*U0)
+    f2(*A0)
+    own(*D0)
+    f2(*U0)
+    f3(*A0)
+    f3(*U0)
+    f1(*D0)
+    f4(*A0)
+    own(*U1)
+    f4(*U0)
+    got_partner(*A0)
     vectors()
     swap_x.wait_recv()
-    norms(x_ref, 0, False)
+    norms(x_ref, 0)
+    f2(*D0)
     make_qkv(0)
-    f3(0, DN)
-    f1(1, UP)
-    heads(False, 0, 2)
-    own(1, DN)
-    heads(False, 2, 4)
-    f2(1, UP)
-    heads(False, 4, 6)
-    f3(1, UP)
-    f4(0, DN)
-    heads(False, 6, 8)
-    f1(1, DN)
-    got_partner(0, UP)
-    got_partner(0, DN)
-    mlp_fwd(0)
-    f2(1, DN)
-    own(1, AO)
+    f3(*D0)
+    heads(0, False, 0, 1)
+    f1(*U1)
+    heads(0, False, 1, 2)
+    f2(*U1)
+    own(*A1)
+    heads(0, False, 2, 4)
+    f4(*D0)
+    got_partner(*U0)
+    got_partner(*D0)
+    swap_cot.start()
+    activate(0, True, 0, 2)
+    f3(*U1)
+    f1(*A1)
+    activate(0, True, 2, 4)
+    own(*D1)
     acc[EV] += mm(ctx[EV], wa[0, :, Q3:FF])
     h1[EV] = (x_ref[EV].astype(F32) + acc[EV] + vec[0, 2:3, :] + vec[0, 5:6, :]).astype(BF)
-    f3(1, DN)
-    f4(1, UP)
-    norms(h1, 1, True)
-    f1(1, AO)
-    f2(1, AO)
-    got_partner(1, UP)
+    f4(*U1)
+    f2(*A1)
+    norms(h1, 1)
+    got_partner(*U1)
+    activate(1, False, 0, 4)
     swap_cot.wait_recv()
-    mlp_a(1, cot_ref)
-    s0(1, DN)
-    f4(1, DN)
-    s1(1, DN)
-    f3(1, AO)
-    got_partner(1, DN)
-    mlp_b(1, cot_ref, True)
-    s0(1, UP)
-    f4(1, AO)
-    s1(1, UP)
-    got_partner(1, AO)
+    down_grad(1, cot_ref)
+    s0(*D1)
+    f3(*A1)
+    f1(*D1)
+    f4(*A1)
+    s1(*D1)
+    f2(*D1)
+    got_partner(*A1)
     make_qkv(1)
     dctx[EV] = mm_nt(cot_ref[EV], wa[1, :, Q3:FF]).astype(BF)
-    heads(True, 0, 4)
-    s2(1, DN)
-    heads(True, 4, 8)
+    f3(*D1)
+    heads(1, True, 0, 2)
+    f4(*D1)
+    heads(1, True, 2, 3)
+    s2(*D1)
+    heads(1, True, 3, 4)
     attn_grads(1, cot_ref)
-    s0(1, AO)
-    s2(1, UP)
+    s0(*A1)
+    got_partner(*D1)
+    mlp_b(1, cot_ref, True, 0, 2)
+    s1(*A1)
+    mlp_b(1, cot_ref, True, 2, 4)
+    s0(*U1)
+    dh[EV] = layer_end(h1, 1, cot_ref, TOK)
+    s1(*U1)
     acc[:SEQ] += mm(ctx[:SEQ], wa[1, :, Q3:FF])
     y_ref[EV] = (h1[:SEQ].astype(F32) + acc[:SEQ] + vec[1, 2:3, :] + vec[1, 5:6, :]).astype(BF)
-    dh[EV] = layer_end(h1, 1, cot_ref, TOK)
-    s1(1, AO)
     small_grads()
-    s0(1, SM)
-
-    norms(x_ref, 0, True)
-    drained(1, DN, 0)
-    drained(1, UP, 0)
-    mlp_a(0, dh)
-    s0(0, DN)
-    s1(1, SM)
-    s1(0, DN)
-    mlp_b(0, dh, False)
-    s0(0, UP)
-    s2(1, AO)
-    make_qkv(0)
+    s0(*V1)
+
+    drained(*D1, 0)
+    down_grad(0, dh)
+    s0(*D0)
+    drained(*U1, 0)
+    mlp_b(0, dh, False, 0, 2)
+    s1(*D0)
+    s2(*A1)
+    mlp_b(0, dh, False, 2, 4)
+    s0(*U0)
+    s1(*V1)
     dctx[EV] = mm_nt(dh[EV], wa[0, :, Q3:FF]).astype(BF)
-    s1(0, UP)
-    heads(True, 0, 4)
-    s2(0, DN)
-    s2(1, SM)
-    heads(True, 4, 8)
-    drained(1, SM, 0)
-    drained(1, AO, 0)
+    s1(*U0)
+    heads(0, True, 0, 2)
+    s2(*U1)
+    s2(*V1)
+    heads(0, True, 2, 4)
+    drained(*V1, 0)
+    drained(*A1, 0)
     attn_grads(0, dh)
-    s0(0, AO)
-    s3(1, SM)
+    s0(*A0)
+    s3(*V1)
     xg_ref[EV] = layer_end(x_ref, 0, dh, SEQ)
-    s1(0, AO)
+    s1(*A0)
     small_grads()
-    s0(0, SM)
-    s2(0, UP)
-    s1(0, SM)
-    for stage, l, w in ((s3, 1, DN), (s3, 1, UP), (s3, 1, AO), (s4, 1, SM), (s2, 0, SM), (s3, 0, DN), (s2, 0, AO),
-                        (s3, 0, UP), (s3, 0, SM), (s4, 0, SM), (s3, 0, AO)):
-        stage(l, w)
+    s0(*V0)
+    s2(*D0)
+    s1(*V0)
+    for stage, at in ((s2, U0), (s3, D1), (s3, A1), (s2, V0), (s3, U1), (s4, V1), (s2, A0), (s3, V0), (s3, D0), (s3, U0),
+                      (s4, V0), (s3, A0)):
+        stage(*at)
     swap_x.wait_send()
     swap_cot.wait_send()
     for w in (DN, UP, AO, SM):
@@ -604,7 +606,7 @@
         c[:, base + half:base + rot] = cos
         p[:, base:base + half] = -sin
         q[:, base + half:base + rot] = sin
-    return np.tile(np.stack([c, p, q]), (1, 2, 1))
+    return np.stack([c, p, q])
 
 
 def solution(mesh):
@@ -629,11 +631,11 @@
             scratch += [v((LAYERS,) + (2,) * (n - i) + (ROWS[w], COLS[w]), F32) for i in range(n + 1)]
         scratch += [v(p.shape, BF) for p in little]
         scratch += [v((LAYERS, 8, DM), F32), v((LAYERS, 1, FF), F32), v((LAYERS, 1, Q3), F32),
-                    v((8, DM), F32), v((1, FF), F32), v((2, 1, Q3), F32)]
+                    v((8, DM), F32), v((1, FF), F32), v((1, Q3), F32)]
         scratch += [v((TOK, DM), BF)] * 2
-        scratch += [v((3, TOK, LN), F32), v((LAYERS, SH, 8, 3 * HD), BF), v((2, SEQ, LN), F32), v((TOK, FF), BF),
-                    v((TOK, FF), F32)]
-        scratch += [v((TOK, DM), BF)] * 4 + [v((DM, TOK), BF)] * 2 + [v((TOK, Q3), BF)] * 2
+        scratch += [v((3, TOK, LN), F32), v((LAYERS, SH, 8, 3 * HD), BF), v((2, SEQ, LN), F32), v((LAYERS, TOK, FF), BF),
+                    v((LAYERS, TOK, FF), F32)]
+        scratch += [v((TOK, DM), BF)] * 4 + [v((LAYERS, DM, TOK), BF)] * 2 + [v((LAYERS, TOK, Q3), BF), v((TOK, Q3), BF)]
         scratch += [v((TOK, DM), BF)] * 2 + [v((TOK, DM), F32)] * 2
         dma = pltpu.SemaphoreType.DMA
         scratch += [dma((6, 4)), dma((LAYERS, 3)), dma((LAYERS, 3, 3, 8)), dma((LAYERS, 3)), dma((LAYERS, 4, 3, 4)),

time: 131 us -> 125 us (0.954)
  Pallas kernels: 130 us -> 124 us
    pallas_call x1, Pallas kernels: 128 us -> 122 us  [device_step(): pl.pallas_call(kernel, out_shape=[sds((SEQ, DM), BF), sds((SEQ, DM), BF),...]
where the time goes in v5:
time: 125 us
  Pallas kernels  124 us (99%)
    pallas_call x1, Pallas kernels, device_step(): pl.pallas_call(kernel, out_shape=[sds((SEQ, DM), BF), sds((SEQ, DM), BF),...  122 us
    pallas_call x1, Pallas kernels, device_step(): pl.pallas_call(finish, out_shape=[sds(p.shape, BF) for p in like], in_spe...  2.53 us

profile of v5, /device:TPU:0, one launch (start us, length us, event | category | flops | bytes accessed | tf_op | source)
XLA Modules:
  0.0 125.2 jit_solution(6246962090769496513)
XLA Ops:
  0.7 121.9 %step.1 = (bf16[256,512]{1,0:T(8,128)(2,1)}, bf16[256,512]{1,0:T(8,128)(2,1)}, bf16[2,32,1536]{2,1,0:T(8,128)(2,1)}, bf16[2,32,512]{2,1,0:T(8,128)(2,1)}, bf16[2...) custom-call(bf16[256,512]{1,0:T(8,128)(2,1)} %bitcast.2, bf16[256,512]{1,0:T(8,128)(2,1)} %bitcast.3, ...), custom_call_target="tpu_custom_call" | custom-call | tf_op jit(solution)/shard_map/step/pallas_call | solution.py:644
  122.5 2.5 %finish.1 = (bf16[1,256,512]{2,1,0:T(8,128)(2,1)}, bf16[1,256,512]{2,1,0:T(8,128)(2,1)}, bf16[2,32]{1,0:T(2,128)(2,1)}, bf16[2,32]{1,0:T(2,128)(2,1)}, bf16[2,32...) custom-call(bf16[256,512]{1,0:T(8,128)(2,1)} %get-tuple-element.21.y, ...), custom_call_target="tpu_custom_call" | custom-call | tf_op jit(solution)/shard_map/finish/pallas_call | solution.py:656

commit v6 on v5

--- a/solution.py
+++ b/solution.py
@@ -25,7 +25,7 @@
 
 
 def routes(w):
-    return ORDERS[:1] if w == SM else ROUTES
+    return ORDERS[2:] if w == SM else ROUTES
 
 
 def axes_of(w):
@@ -277,38 +277,37 @@
     def heads(l, bwd, lo, hi):
         lane = lax.broadcasted_iota(jnp.int32, (1, LN), 1)
         sides = [(lane < HD).astype(F32), (lane >= HD).astype(F32)]
-        row, key = (lax.broadcasted_iota(jnp.int32, (SEQ, SEQ), t) for t in range(2))
-        causal = row >= key
+        row, key = (lax.broadcasted_iota(jnp.int32, (TOK, SEQ), t) for t in range(2))
+        causal = lax.rem(row, SEQ) >= key
+
+        def stacked(v, scale):
+            return jnp.concatenate([v * (side * scale).astype(BF) for side in sides])
+
+        def along(v):
+            return jnp.concatenate([v[:SEQ], v[SEQ:]], axis=1)
 
         def pair(seq, col):
             rows = slice(SEQ * seq, SEQ * seq + SEQ)
             q, k, v = (qkv[l, rows, pl.ds(col + DM * t, LN)] for t in range(3))
-            dc = dctx[rows, pl.ds(col, LN)] if bwd else None
-            out = dq = dk = dv = 0.0
-            for side in sides:
-                one, eighth = side.astype(BF), (side * 0.125).astype(BF)
-                qm = q * eighth
-                sc = jnp.where(causal, mm_nt(qm, k), -1e30)
-                e = jnp.exp(sc - row_of(jnp.max, sc))
-                p = e * (1.0 / row_of(jnp.sum, e))
-                pb = p.astype(BF)
-                out += mm(pb, v * one)
-                if bwd:
-                    dcm = dc * one
-                    dp = mm_nt(dcm, v).astype(BF).astype(F32)
-                    ds = (p * (dp - row_of(jnp.sum, dp * p))).astype(BF)
-                    dq += mm(ds, k * eighth)
-                    dk += mm_tn(ds, qm)
-                    dv += mm_tn(pb, dcm)
-            ctx[rows, pl.ds(col, LN)] = out.astype(BF)
-            if bwd:
-                for t, d in enumerate((dq, dk, dv)):
-                    d = d.astype(BF).astype(F32)
-                    if t < 2:
-                        d = rope(d, True, SEQ)
-                    if seq == 0:
-                        gqb[0:1, pl.ds(col + DM * t, LN)] = col_sum(d)
-                    dqkv[rows, pl.ds(col + DM * t, LN)] = d.astype(BF)
+            qs = stacked(q, 0.125)
+            sc = jnp.where(causal, mm_nt(qs, k), -1e30)
+            e = jnp.exp(sc - row_of(jnp.max, sc))
+            p = e * (1.0 / row_of(jnp.sum, e))
+            pb = p.astype(BF)
+            ctx[rows, pl.ds(col, LN)] = mm(along(pb), stacked(v, 1.0)).astype(BF)
+            if not bwd:
+                return
+            ds_ = stacked(dctx[rows, pl.ds(col, LN)], 1.0)
+            dp = mm_nt(ds_, v).astype(BF).astype(F32)
+            ds = (p * (dp - row_of(jnp.sum, dp * p))).astype(BF)
+            grads = (mm(along(ds), stacked(k, 0.125)), mm_tn(ds, qs), mm_tn(pb, ds_))
+            for t, d in enumerate(grads):
+                d = d.astype(BF).astype(F32)
+                if t < 2:
+                    d = rope(d, True, SEQ)
+                if seq == 0:
+                    gqb[0:1, pl.ds(col + DM * t, LN)] = col_sum(d)
+                dqkv[rows, pl.ds(col + DM * t, LN)] = d.astype(BF)
 
         def body(j, carry):
             col = pl.multiple_of(j * LN, LN)
@@ -547,20 +546,20 @@
     heads(0, True, 0, 2)
     s2(*U1)
     s2(*V1)
+    s2(*D0)
     heads(0, True, 2, 4)
+    xg_ref[EV] = layer_end(x_ref, 0, dh, SEQ)
     drained(*V1, 0)
+    small_grads()
+    s0(*V0)
     drained(*A1, 0)
     attn_grads(0, dh)
     s0(*A0)
+    s1(*V0)
     s3(*V1)
-    xg_ref[EV] = layer_end(x_ref, 0, dh, SEQ)
     s1(*A0)
-    small_grads()
-    s0(*V0)
-    s2(*D0)
-    s1(*V0)
-    for stage, at in ((s2, U0), (s3, D1), (s3, A1), (s2, V0), (s3, U1), (s4, V1), (s2, A0), (s3, V0), (s3, D0), (s3, U0),
-                      (s4, V0), (s3, A0)):
+    for stage, at in ((s2, V0), (s2, U0), (s3, D1), (s3, A1), (s3, V0), (s2, A0), (s3, U1), (s4, V1), (s3, D0),
+                      (s3, U0), (s4, V0), (s3, A0)):
         stage(*at)
     swap_x.wait_send()
     swap_cot.wait_send()

time: 125 us -> 122 us (0.976)
  Pallas kernels: 124 us -> 121 us
    pallas_call x1, Pallas kernels: 122 us -> 118 us  [device_step(): pl.pallas_call(kernel, out_shape=[sds((SEQ, DM), BF), sds((SEQ, DM), BF),...]
where the time goes in v6:
time: 122 us; the launch traced here: 121 us
  Pallas kernels  121 us (99%)
    pallas_call x1, Pallas kernels, device_step(): pl.pallas_call(kernel, out_shape=[sds((SEQ, DM), BF), sds((SEQ, DM), BF),...  118 us
    pallas_call x1, Pallas kernels, device_step(): pl.pallas_call(finish, out_shape=[sds(p.shape, BF) for p in like], in_spe...  2.53 us

profile of v6, /device:TPU:0, one launch (start us, length us, event | category | flops | bytes accessed | tf_op | source)
XLA Modules:
  0.0 121.4 jit_solution(13173563429256137015)
XLA Ops:
  0.7 118.1 %step.1 = (bf16[256,512]{1,0:T(8,128)(2,1)}, bf16[256,512]{1,0:T(8,128)(2,1)}, bf16[2,32,1536]{2,1,0:T(8,128)(2,1)}, bf16[2,32,512]{2,1,0:T(8,128)(2,1)}, bf16[2...) custom-call(bf16[256,512]{1,0:T(8,128)(2,1)} %bitcast.2, bf16[256,512]{1,0:T(8,128)(2,1)} %bitcast.3, ...), custom_call_target="tpu_custom_call" | custom-call | tf_op jit(solution)/shard_map/step/pallas_call | solution.py:643
  118.8 2.5 %finish.1 = (bf16[1,256,512]{2,1,0:T(8,128)(2,1)}, bf16[1,256,512]{2,1,0:T(8,128)(2,1)}, bf16[2,32]{1,0:T(2,128)(2,1)}, bf16[2,32]{1,0:T(2,128)(2,1)}, bf16[2,32...) custom-call(bf16[256,512]{1,0:T(8,128)(2,1)} %get-tuple-element.21.y, ...), custom_call_target="tpu_custom_call" | custom-call | tf_op jit(solution)/shard_map/finish/pallas_call | solution.py:655

commit v7 on v6

--- a/solution.py
+++ b/solution.py
@@ -17,8 +17,8 @@
 AO, UP, DN, SM = range(4)
 ORDERS = ((1, 2, 4), (2, 4, 1), (4, 1, 2))
 CHIP_AXES = [4, 2, 1]
-CUTS = ((0, 384, 1152, FF), (0, 384, 1152, FF), (0, SH, 80, LN))
-WIDE = (0, 384, 1152, WIDTH)
+CUTS = ((0, 256, 1024, FF), (0, 256, 1024, FF), (0, SH, 80, LN))
+WIDE = (0, 256, 1024, WIDTH)
 ROUTES = ((1, 2), (2, 1))
 ALL, EV = slice(None), ...
 TOK = 2 * SEQ

time: 122 us -> 120 us (0.984)
  no operation moved by 1% of the time
where the time goes in v7:
time: 120 us
  Pallas kernels  120 us (100%)
    pallas_call x1, Pallas kernels, device_step(): pl.pallas_call(kernel, out_shape=[sds((SEQ, DM), BF), sds((SEQ, DM), BF),...  117 us
    pallas_call x1, Pallas kernels, device_step(): pl.pallas_call(finish, out_shape=[sds(p.shape, BF) for p in like], in_spe...  2.53 us

profile of v7, /device:TPU:0, one launch (start us, length us, event | category | flops | bytes accessed | tf_op | source)
XLA Modules:
  0.0 120.3 jit_solution(4858436677904526503)
XLA Ops:
  0.7 117.0 %step.1 = (bf16[256,512]{1,0:T(8,128)(2,1)}, bf16[256,512]{1,0:T(8,128)(2,1)}, bf16[2,32,1536]{2,1,0:T(8,128)(2,1)}, bf16[2,32,512]{2,1,0:T(8,128)(2,1)}, bf16[2...) custom-call(bf16[256,512]{1,0:T(8,128)(2,1)} %bitcast.2, bf16[256,512]{1,0:T(8,128)(2,1)} %bitcast.3, ...), custom_call_target="tpu_custom_call" | custom-call | tf_op jit(solution)/shard_map/step/pallas_call | solution.py:643
  117.6 2.5 %finish.1 = (bf16[1,256,512]{2,1,0:T(8,128)(2,1)}, bf16[1,256,512]{2,1,0:T(8,128)(2,1)}, bf16[2,32]{1,0:T(2,128)(2,1)}, bf16[2,32]{1,0:T(2,128)(2,1)}, bf16[2,32...) custom-call(bf16[256,512]{1,0:T(8,128)(2,1)} %get-tuple-element.21.y, ...), custom_call_target="tpu_custom_call" | custom-call | tf_op jit(solution)/shard_map/finish/pallas_call | solution.py:655

commit v8 on v7

--- a/solution.py
+++ b/solution.py
@@ -17,8 +17,8 @@
 AO, UP, DN, SM = range(4)
 ORDERS = ((1, 2, 4), (2, 4, 1), (4, 1, 2))
 CHIP_AXES = [4, 2, 1]
-CUTS = ((0, 256, 1024, FF), (0, 256, 1024, FF), (0, SH, 80, LN))
-WIDE = (0, 256, 1024, WIDTH)
+CUTS = ((0, 128, 896, FF), (0, 128, 896, FF), (0, SH, 80, LN))
+WIDE = (0, 128, 896, WIDTH)
 ROUTES = ((1, 2), (2, 1))
 ALL, EV = slice(None), ...
 TOK = 2 * SEQ

time: 120 us -> 121 us (level)
  no operation moved by 1% of the time
where the time goes in v8:
time: 121 us
  Pallas kernels  120 us (99%)
    pallas_call x1, Pallas kernels, device_step(): pl.pallas_call(kernel, out_shape=[sds((SEQ, DM), BF), sds((SEQ, DM), BF),...  118 us
    pallas_call x1, Pallas kernels, device_step(): pl.pallas_call(finish, out_shape=[sds(p.shape, BF) for p in like], in_spe...  2.53 us

profile of v8, /device:TPU:0, one launch (start us, length us, event | category | flops | bytes accessed | tf_op | source)
XLA Modules:
  0.0 121.2 jit_solution(16920139804607558323)
XLA Ops:
  0.7 117.8 %step.1 = (bf16[256,512]{1,0:T(8,128)(2,1)}, bf16[256,512]{1,0:T(8,128)(2,1)}, bf16[2,32,1536]{2,1,0:T(8,128)(2,1)}, bf16[2,32,512]{2,1,0:T(8,128)(2,1)}, bf16[2...) custom-call(bf16[256,512]{1,0:T(8,128)(2,1)} %bitcast.2, bf16[256,512]{1,0:T(8,128)(2,1)} %bitcast.3, ...), custom_call_target="tpu_custom_call" | custom-call | tf_op jit(solution)/shard_map/step/pallas_call | solution.py:643
  118.5 2.5 %finish.1 = (bf16[1,256,512]{2,1,0:T(8,128)(2,1)}, bf16[1,256,512]{2,1,0:T(8,128)(2,1)}, bf16[2,32]{1,0:T(2,128)(2,1)}, bf16[2,32]{1,0:T(2,128)(2,1)}, bf16[2,32...) custom-call(bf16[256,512]{1,0:T(8,128)(2,1)} %get-tuple-element.21.y, ...), custom_call_target="tpu_custom_call" | custom-call | tf_op jit(solution)/shard_map/finish/pallas_call | solution.py:655
